TPU v7x, 128 devices: a whole 4x4x4 slice. The times are simulated.
128 devices in a mesh: seq: 32 (over x, y, core), head: 4 (over z).
Axes of the slice: x: 4, y: 4, z: 4, core: 2. Of those that a mesh axis runs over, the one named last changes fastest.
Arguments:
- queries: bfloat16 [4096, 8192], P('seq', 'head'), may hold values from -2.5 to 2.5
- keys: bfloat16 [4096, 8192], P('seq', 'head'), may hold values from -2.5 to 2.5
- values: bfloat16 [4096, 4096], P('seq', 'head'), may hold values from -2.5 to 2.5
- out_grad: bfloat16 [4096, 4096], P('seq', 'head'), may hold values from -2.5 to 2.5
- log_gate: float32 [64, 4096], P('head', 'seq'), may hold values from -1 to 0
- level_weight: float32 [6, 64, 4096], P(None, 'head', 'seq'), may hold values from 0.25 to 2
- doc_start: int32 [4096], P('seq'), may hold values 0 or 1
Outputs:
- grad_queries: bfloat16 [4096, 8192], P('seq', 'head')
- grad_keys: bfloat16 [4096, 8192], P('seq', 'head')
- grad_values: bfloat16 [4096, 4096], P('seq', 'head')
- grad_level_weight: float32 [6, 64, 4096], P(None, 'head', 'seq')
- grad_log_gate: float32 [64, 4096], P('head', 'seq')
All inputs are finite; a program needn't handle non-finite values. No bound on the sum of `doc_start` on one device may be relied on, other than what follows from the above.
Results may differ from a plain program's by a relative error of at most 0.0027.
Values sent between devices are 32-bit elements; how exact they have to be, the bound alone decides.
A program may use at most 128 MiB of HBM per device.

v0:
```python
import jax
import jax.numpy as jnp
from jax import lax
from jax.sharding import Mesh
from jax.sharding import PartitionSpec as P

SPAN = 64
SEQ = ("seq_0", "seq_1", "seq_2")
SEQ_HEAD = ("seq_0", "seq_1", "seq_2", "head")


exact_mode = lax.Precision.HIGHEST


def from_partner(block, axis, stride):
    count = lax.axis_size(axis)
    route = []
    for low in range(count):
        high = low | 1 << stride
        if high != low and high < count:
            route += [(low, high), (high, low)]
    return lax.ppermute(block, axis, route)


def from_everyone(shard, axis):
    copies = jnp.broadcast_to(shard, (lax.axis_size(axis), *shard.shape))
    return lax.all_to_all(copies, axis, split_axis=0, concat_axis=0, tiled=True)


def joined_by_halves(pieces, combine):
    while len(jax.tree.leaves(pieces)[0]) > 1:
        pieces = jax.vmap(combine)(*(pieces[side::2] for side in (0, 1)))
    return pieces[0]


def carried_in(shard, axis, combine, identity):
    devices, position = (lax.axis_size(axis), lax.axis_index(axis))
    passed = jnp.arange(devices) > position

    def kept(part, zero, own):
        part = jnp.where(
            passed.reshape(-1, *(1 for _ in own.shape)), part, jnp.asarray(zero, own.dtype)
        )
        return part[::-1]

    pieces = from_everyone(shard, axis)
    return joined_by_halves(kept(pieces, identity, shard), combine)


def one_axis_at_a_time(shard, axes):
    for axis in axes:
        shard = lax.psum(shard, axis)
    return shard


def total_combine(earlier_part, later_part):
    return earlier_part + later_part


def level_table(count, span_bits, levels):
    positions = jnp.arange(count, dtype=jnp.int32)
    crossed = jnp.bitwise_xor(positions[:, None], positions[None, :])
    level = jnp.zeros((count, count), jnp.int32)
    for bit in range(span_bits + 1):
        level = level + (crossed >= 2**bit).astype(jnp.int32)
    return jnp.minimum(level, levels - 1)


def shards(queries, keys, values, out_grad, log_gate, level_weight, doc_start):
    tok_dev = queries.shape[0]
    heads_dev = log_gate.shape[0]
    levels = level_weight.shape[0]
    spans = tok_dev // SPAN
    span_bits = spans.bit_length() - 1
    seq_bits = lax.axis_size(SEQ).bit_length() - 1
    state_k = queries.shape[1] // heads_dev
    state_v = values.shape[1] // heads_dev
    query_blk = queries.reshape(spans, SPAN, heads_dev, state_k)
    key_blk = keys.reshape(spans, SPAN, heads_dev, state_k)
    value_blk = values.reshape(spans, SPAN, heads_dev, state_v)
    grad_blk = out_grad.reshape(spans, SPAN, heads_dev, state_v)
    query_f32 = query_blk.astype(jnp.float32)
    key_f32 = key_blk.astype(jnp.float32)
    value_f32 = value_blk.astype(jnp.float32)
    grad_f32 = grad_blk.astype(jnp.float32)
    gates = log_gate.reshape(heads_dev, spans, SPAN)
    starts = doc_start.reshape(spans, SPAN)
    cum_gate = jnp.cumsum(gates, axis=2)
    cum_reset = jnp.cumsum(starts, axis=1)
    positions = jnp.arange(SPAN)
    causal = positions[:, None] >= positions[None, :]
    valid_pair = (causal[None] & (cum_reset[:, :, None] == cum_reset[:, None, :]))[None]
    gate_diff = cum_gate[:, :, :, None] - cum_gate[:, :, None, :]
    decay_in = jnp.where(valid_pair, jnp.exp(jnp.where(valid_pair, gate_diff, 0.0)), 0.0)
    from_start = jnp.exp(cum_gate) * (cum_reset == 0).astype(jnp.float32)[None]
    to_end = (
        jnp.exp(cum_gate[:, :, -1:] - cum_gate)
        * (cum_reset == cum_reset[:, -1:]).astype(jnp.float32)[None]
    )
    span_log = cum_gate[:, :, -1]
    span_dead = (cum_reset[:, -1] > 0).astype(jnp.int32)
    weights = level_weight.reshape(levels, heads_dev, spans, SPAN)
    scores = jnp.einsum("cthd,cshd->hcts", query_blk, key_blk, preferred_element_type=jnp.float32)
    grad_dot = jnp.einsum(
        "cthe,cshe->hcts", grad_blk, value_blk, preferred_element_type=jnp.float32
    )
    weighted = decay_in * weights[0][:, :, :, None]
    prob_mix = (weighted * scores).astype(jnp.bfloat16)
    grad_mix = (weighted * grad_dot).astype(jnp.bfloat16)
    intra_sum = jnp.sum(decay_in * scores * grad_dot, axis=3)
    end_col = to_end.transpose(1, 2, 0)[:, :, :, None]
    key_end = key_f32 * end_col
    span_state = jnp.einsum("cshd,cshe->chde", key_end, value_f32, precision=exact_mode)
    cum_log = jnp.cumsum(span_log, axis=1)
    cum_dead = jnp.cumsum(span_dead)
    lead_log = cum_log - span_log
    lead_dead = cum_dead - span_dead
    span_index = jnp.arange(spans)
    same = (span_index[:, None] > span_index[None, :]) & (lead_dead[:, None] == cum_dead[None, :])
    gap = lead_log[:, :, None] - cum_log[:, None, :]
    between = jnp.where(same[None], jnp.exp(jnp.where(same[None], gap, 0.0)), 0.0)
    table = level_table(spans, span_bits, levels)
    level_hot = (table[None] == jnp.arange(levels, dtype=jnp.int32)[:, None, None]).astype(
        jnp.float32
    )
    local_fwd = jnp.einsum(
        "hjs,ljs,shde->jlhde", between, level_hot, span_state, precision=exact_mode
    )
    lead_decay = jnp.exp(lead_log) * (lead_dead == 0).astype(jnp.float32)[None]
    tail_same = (cum_dead[-1] == cum_dead)[None]
    tail_decay = jnp.where(
        tail_same, jnp.exp(jnp.where(tail_same, cum_log[:, -1:] - cum_log, 0.0)), 0.0
    )
    dev_decay = jnp.exp(cum_log[:, -1]) * (cum_dead[-1] == 0).astype(jnp.float32)
    dev_state = jnp.einsum("hc,chde->hde", tail_decay, span_state, precision=exact_mode)
    cross_level = [min(span_bits + 1 + bit, levels - 1) for bit in range(seq_bits)]
    place = lax.axis_index(SEQ)
    upper_bits = [(place >> bit & 1).astype(jnp.float32) for bit in range(seq_bits)]
    incoming = [jnp.zeros_like(dev_state) for level_idx in range(levels)]
    block_state, block_decay, inner_decay = (dev_state, dev_decay, jnp.ones_like(dev_decay))
    for bit in range(seq_bits):
        other_state, other_decay = from_partner((block_state, block_decay), SEQ, bit)
        upper = upper_bits[bit] > 0.5
        incoming[cross_level[bit]] = incoming[cross_level[bit]] + jnp.where(
            upper, inner_decay[:, None, None] * other_state, 0.0
        )
        block_state = jnp.where(
            upper,
            block_decay[:, None, None] * other_state + block_state,
            other_decay[:, None, None] * block_state + other_state,
        )
        inner_decay = inner_decay * jnp.where(upper, other_decay, 1.0)
        block_decay = block_decay * other_decay
    prev_state = local_fwd + lead_decay.T[:, None, :, None, None] * jnp.stack(incoming)[None]
    query_state = jnp.einsum("cthd,clhde->hctle", query_f32, prev_state, precision=exact_mode)
    lam_start = weights.transpose(1, 2, 3, 0) * from_start[:, :, :, None]
    out_in = jnp.einsum("hctle,hctl->cthe", query_state, lam_start, precision=exact_mode)
    level_in = (
        jnp.einsum("hctle,cthe->lhct", query_state, grad_f32, precision=exact_mode)
        * from_start[None]
    )
    grad_weighted = lam_start[:, :, :, :, None] * grad_f32.transpose(2, 0, 1, 3)[:, :, :, None, :]
    query_grad_in = jnp.einsum("hctle,clhde->cthd", grad_weighted, prev_state, precision=exact_mode)
    out_loc = jnp.einsum("hcts,cshe->cthe", prob_mix, value_blk, preferred_element_type=jnp.float32)
    query_grad_loc = jnp.einsum(
        "hcts,cshd->cthd", grad_mix, key_blk, preferred_element_type=jnp.float32
    )
    outputs = out_loc + out_in
    grad_query = (
        (query_grad_loc + query_grad_in).astype(jnp.bfloat16).reshape(tok_dev, heads_dev * state_k)
    )
    level_zero = (jnp.arange(levels) == 0).astype(jnp.float32)
    grad_level = (level_in + level_zero[:, None, None, None] * intra_sum[None]).reshape(
        levels, heads_dev, tok_dev
    )
    query_start = query_f32 * from_start.transpose(1, 2, 0)[:, :, :, None]
    lam_grad = weights.transpose(2, 3, 1, 0)[:, :, :, :, None] * grad_f32[:, :, :, None, :]
    back_local = jnp.einsum("cthd,cthle->clhde", query_start, lam_grad, precision=exact_mode)
    later_local = jnp.einsum(
        "hts,lts,tlhde->shde", between, level_hot, back_local, precision=exact_mode
    )
    dev_back = jnp.einsum("hc,clhde->lhde", lead_decay, back_local, precision=exact_mode)
    later_sum = jnp.zeros_like(dev_state)
    carry_levels = sorted(set(cross_level))
    block_state = jnp.stack([dev_back[level_idx] for level_idx in carry_levels])
    block_decay, inner_decay = (dev_decay, jnp.ones_like(dev_decay))
    for bit in range(seq_bits):
        other_state, other_decay = from_partner((block_state, block_decay), SEQ, bit)
        upper = upper_bits[bit] > 0.5
        slot = carry_levels.index(cross_level[bit])
        later_sum = later_sum + jnp.where(
            upper, 0.0, inner_decay[:, None, None] * other_state[slot]
        )
        block_state = jnp.where(
            upper,
            other_state + other_decay[None, :, None, None] * block_state,
            block_state + block_decay[None, :, None, None] * other_state,
        )
        inner_decay = inner_decay * jnp.where(upper, 1.0, other_decay)
        block_decay = block_decay * other_decay
    after_state = later_local + tail_decay.T[:, :, None, None] * later_sum[None]
    key_grad_in = jnp.einsum(
        "cshe,chde->cshd", value_f32 * end_col, after_state, precision=exact_mode
    )
    value_grad_in = jnp.einsum("cshd,chde->cshe", key_end, after_state, precision=exact_mode)
    key_grad_loc = jnp.einsum(
        "hcts,cthd->cshd", grad_mix, query_blk, preferred_element_type=jnp.float32
    )
    value_grad_loc = jnp.einsum(
        "hcts,cthe->cshe", prob_mix, grad_blk, preferred_element_type=jnp.float32
    )
    value_grad = value_grad_loc + value_grad_in
    grad_key = (
        (key_grad_loc + key_grad_in).astype(jnp.bfloat16).reshape(tok_dev, heads_dev * state_k)
    )
    grad_value = value_grad.astype(jnp.bfloat16).reshape(tok_dev, heads_dev * state_v)
    drift_term = jnp.sum(grad_f32 * outputs, axis=3) - jnp.sum(value_f32 * value_grad, axis=3)
    drift_term = drift_term.reshape(tok_dev, heads_dev).T
    local_tail = lax.cumsum(drift_term, axis=1, reverse=True)
    dev_total = local_tail[:, 0]
    count = heads_dev * tok_dev * lax.axis_size(SEQ) * lax.axis_size("head")
    later_total = carried_in(dev_total, SEQ, total_combine, jnp.zeros_like(dev_total))
    gate_grad = local_tail + later_total[:, None]
    squares = one_axis_at_a_time(jnp.sum(gate_grad * gate_grad), SEQ_HEAD)
    scale_factor = jnp.minimum(1.0, lax.rsqrt(squares / count + 1e-06))
    return (grad_query, grad_key, grad_value, grad_level, gate_grad * scale_factor)


def solution(mesh):
    finer = Mesh(
        mesh.devices.reshape(4, 4, 2, mesh.shape["head"]), ("seq_0", "seq_1", "seq_2", "head")
    )
    placed = (
        P(SEQ, "head"),
        P(SEQ, "head"),
        P(SEQ, "head"),
        P(SEQ, "head"),
        P("head", SEQ),
        P(None, "head", SEQ),
        P(SEQ),
    )
    return jax.shard_map(
        shards,
        mesh=finer,
        in_specs=placed,
        out_specs=(
            P(SEQ, "head"),
            P(SEQ, "head"),
            P(SEQ, "head"),
            P(None, "head", SEQ),
            P("head", SEQ),
        ),
        check_vma=False,
    )
```

profile of v0, /device:TPU:0, one launch (start us, length us, event | category | flops | bytes accessed | tf_op | source)
XLA Modules:
  0.0 396.6 jit_solution(5546207695720665487)
XLA Ops:
  9.4 5.9 %fusion.17 = f32[2,6,16,128,64]{3,4,1,2,0:T(8,128)S(1)} fusion(f32[2,64,16,64]{1,3,2,0:T(8,128)S(1)} %get-tuple-element.21, f32[2,64,16,6]{1,3,2,0:T(8,128)S(1)} %copy.206, f32[2,64,16]{1,2,0:T(8,128)S(1)} %get-tuple-element.32, bf16[2,64,16,128]{3,2,1,0:T(8,128)(2,1)S(1)} %bitcast.172), kind=kOutput, calls=%fused_computation.21 | convolution fusion | flops 1209270272 | bytes 7397376 | tf_op jit(solution)/shard_map/cthd,cthle->clhde/dot_general | solution.py:178
  15.3 23.4 %fusion.11 = f32[16,1,6,128,64]{3,1,4,2,0:T(1,128)S(1)} fusion(f32[16,2,1,1,1]{1,2,4,3,0:T(1,128)S(1)} %copy.236, f32[2,6,16,128,64]{3,4,1,2,0:T(8,128)S(1)} %fusion.17), kind=kOutput, calls=%fused_computation.14 | convolution fusion | flops 18874368 | bytes 9437312 | tf_op jit(solution)/shard_map/hc,clhde->lhde/dot_general | solution.py:182
  48.4 3.6 add_select_fusion.3
  59.9 40.0 %collective-permute-done.3 = f32[16]{0:T(128)S(1)} collective-permute-done((f32[16]{0:T(128)S(1)}, f32[16]{0:T(128)S(1)}, u32[]{:S(2)}, u32[]{:S(2)}) %collective-permute-start.3) | collective-permute-done | bytes 96 | tf_op jit(solution)/shard_map/ppermute | solution.py:22
  99.8 4.4 %add_select_fusion.2 = f32[4,16,128,64]{2,3,1,0:T(8,128)} fusion(f32[4,16,128,64]{2,3,1,0:T(8,128)} %add_select_fusion.3, f32[4,16,128,64]{2,3,1,0:T(8,128)} %collective-permute-done.10, f32[16]{0:T(128)S(1)} %fusion.102, f32[16]{0:T(128)S(1)} %collective-permute-done.3, pred[]{:T(512)S(6)} %gt.58), kind=kLoop, calls=%fused_computation.24 | loop fusion | flops 2621440 | bytes 6291585 | tf_op jit(solution)/shard_map/jit(_where)/select_n | solution.py:194
  104.2 15.0 %collective-permute-start.11 = (f32[4,16,128,64]{2,3,1,0:T(8,128)}, f32[4,16,128,64]{2,3,1,0:T(8,128)}, u32[]{:S(2)}, u32[]{:S(2)}) collective-permute-start(f32[4,16,128,64]{2,3,1,0:T(8,128)} %add_select_fusion.2), channel_id=1, source_target_pairs={{0,16},{16,0},{4,20},{20,4},{8,24},{24,8},{12,28},{28,12},{32,48},... | collective-permute-start | bytes 6291464 | tf_op jit(solution)/shard_map/ppermute | solution.py:22
  128.5 47.2 %collective-permute-done.5 = f32[16]{0:T(128)S(1)} collective-permute-done((f32[16]{0:T(128)S(1)}, f32[16]{0:T(128)S(1)}, u32[]{:S(2)}, u32[]{:S(2)}) %collective-permute-start.5) | collective-permute-done | bytes 96 | tf_op jit(solution)/shard_map/ppermute | solution.py:22
  186.8 7.0 %collective-permute-done.4 = f32[16,128,64]{1,2,0:T(8,128)S(1)} collective-permute-done((f32[16,128,64]{1,2,0:T(8,128)S(1)}, f32[16,128,64]{1,2,0:T(8,128)S(1)}, u32[]{:S(2)}, u32[]{:S(2)}) %collective-permute-start.4) | collective-permute-done | bytes 524320 | tf_op jit(solution)/shard_map/ppermute | solution.py:22
  196.3 4.4 %add_select_fusion.1 = f32[4,16,128,64]{2,3,1,0:T(8,128)} fusion(f32[4,16,128,64]{2,3,1,0:T(8,128)} %add_select_fusion.2, f32[4,16,128,64]{2,3,1,0:T(8,128)} %collective-permute-done.11, f32[16]{0:T(128)S(1)} %mul.465, f32[16]{0:T(128)S(1)} %collective-permute-done.5, pred[]{:T(512)S(6)} %gt.59), kind=kLoop, calls=%fused_computation.23 | loop fusion | flops 2621440 | bytes 6291585 | tf_op jit(solution)/shard_map/jit(_where)/select_n | solution.py:194
  202.9 6.7 %collective-permute-done.6 = f32[16,128,64]{1,2,0:T(8,128)S(1)} collective-permute-done((f32[16,128,64]{1,2,0:T(8,128)S(1)}, f32[16,128,64]{1,2,0:T(8,128)S(1)}, u32[]{:S(2)}, u32[]{:S(2)}) %collective-permute-start.6) | collective-permute-done | bytes 524320 | tf_op jit(solution)/shard_map/ppermute | solution.py:22
  212.9 13.0 %fusion.25 = f32[16,2,128,64]{2,1,3,0:T(2,128)S(1)} fusion(f32[2,6,16,128,64]{3,4,1,2,0:T(8,128)S(1)} %bitcast.165, f32[2,2,16]{1,0,2:T(2,128)S(1)} %select_bitcast_fusion, f32[2,2,6]{2,1,0:T(2,128)S(1)} %fusion.83), kind=kOutput, calls=%fused_computation.27 | convolution fusion | flops 37749120 | bytes 7340384 | tf_op jit(solution)/shard_map/hts,lts,tlhde->shde/dot_general | solution.py:179
  225.9 37.2 %collective-permute-done.8 = f32[16,128,64]{1,2,0:T(8,128)S(1)} collective-permute-done((f32[16,128,64]{1,2,0:T(8,128)S(1)}, f32[16,128,64]{1,2,0:T(8,128)S(1)}, u32[]{:S(2)}, u32[]{:S(2)}) %collective-permute-start.8) | collective-permute-done | bytes 524320 | tf_op jit(solution)/shard_map/ppermute | solution.py:22
  265.5 11.0 %stack.25 = f32[6,16,128,64]{2,0,3,1:T(8,128)} concatenate(f32[2,16,128,64]{2,0,3,1:T(2,128)} %stack.20, f32[1,16,128,64]{2,0,3,1:T(1,128)} %bitcast.180, f32[1,16,128,64]{2,0,3,1:T(1,128)} %bitcast.177, f32[1,16,128,64]{2,0,3,1:T(1,128)} %bitcast.178, f32[1,16,128,64]{2,0,3,1:T(1,128)} %bitcast.179), dimensions={0} | concatenate | bytes 6291456 | tf_op jit(solution)/shard_map/stack | solution.py:154
  276.5 10.6 %bitcast_add_fusion = f32[2,6,16,128,64]{3,1,4,0,2:T(8,128)S(1)} fusion(f32[6,16,128,64]{2,0,3,1:T(8,128)} %stack.25, f32[2,16]{0,1:T(8,128)S(1)} %copy.194, f32[2,16,128,64,1]{2,3,1,0,4:T(8,128)S(1)} %bitcast.176, f32[2,2,16]{1,0,2:T(2,128)S(1)} %select_bitcast_fusion, f32[2,2,6]{2,1,0:T(2,128)S(1)} %fusion.83), kind=kOutput, calls=%fused_computation | convolution fusion | flops 40894848 | bytes 10486240 | tf_op jit(solution)/shard_map/hjs,ljs,shde->jlhde/dot_general | solution.py:126
  287.2 4.5 %add_select_fusion = f32[4,16,128,64]{2,3,1,0:T(8,128)} fusion(f32[4,16,128,64]{2,3,1,0:T(8,128)} %add_select_fusion.1, f32[4,16,128,64]{2,3,1,0:T(8,128)} %collective-permute-done.12, f32[16]{0:T(128)S(1)} %mul.473, f32[16]{0:T(128)S(1)} %collective-permute-done.7, pred[]{:T(512)S(6)} %gt.60), kind=kLoop, calls=%fused_computation.22 | loop fusion | flops 2621440 | bytes 6291585 | tf_op jit(solution)/shard_map/jit(_where)/select_n | solution.py:194
  292.7 5.9 %fusion.3 = (f32[16,2,64,6]{2,3,1,0:T(8,128)S(1)}, f32[16,2,6,64,64]{4,3,2,1,0:T(8,128)}) fusion(f32[16,2,64,64]{2,3,1,0:T(8,128)S(1)} %copy-done.11, bf16[2,64,16,128,1]{3,2,1,0,4:T(8,128)(2,1)S(1)} %copy-done.14, f32[2,6,16,128,64]{3,1,4,0,2:T(8,128)S(1)} %bitcast_add_fusion), kind=kOutput, calls=%fused_computation.6 | convolution fusion | flops 1209520128 | bytes 10534912 | tf_op jit(solution)/shard_map/cthd,clhde->hctle/dot_general | solution.py:155
  298.8 8.4 %fusion.20 = f32[2,64,16,128]{3,1,2,0:T(8,128)S(1)} fusion(f32[16,2,64,64]{3,2,0,1:T(8,128)S(1)} %copy-done.13, f32[16,2,64,6]{2,3,0,1:T(8,128)S(1)} %copy.199, f32[2,6,16,128,64]{3,1,4,0,2:T(8,128)S(1)} %bitcast_add_fusion), kind=kOutput, calls=%fused_computation.26 | convolution fusion | flops 1208745984 | bytes 7913472 | tf_op jit(solution)/shard_map/hctle,clhde->cthd/dot_general | solution.py:163
  309.5 4.2 %fusion.2 = f32[2,64,16,64]{1,3,0,2:T(8,128)S(1)} fusion(f32[16,2,6,64,64]{4,3,2,1,0:T(8,128)} %get-tuple-element.47, f32[2,64,16,6]{1,3,0,2:T(8,128)S(1)} %copy.267), kind=kLoop, calls=%fused_computation.4 | loop fusion | flops 1441792 | bytes 3719168
  314.1 22.4 %collective-permute-done.13 = f32[4,16,128,64]{2,3,1,0:T(8,128)} collective-permute-done((f32[4,16,128,64]{2,3,1,0:T(8,128)}, f32[4,16,128,64]{2,3,1,0:T(8,128)}, u32[]{:S(2)}, u32[]{:S(2)}) %collective-permute-start.13) | collective-permute-done | bytes 2097184 | tf_op jit(solution)/shard_map/ppermute | solution.py:22
  342.7 5.0 %all-to-all-start = ((f32[32,1,16]{2,1,0:T(1,128)}), f32[32,1,16]{2,1,0:T(1,128)S(1)}, u32[]{:S(2)}, u32[]{:S(2)}) async-start(f32[32,1,16]{2,1,0:T(1,128)} %broadcast_in_dim.166), calls=%async_computation | async-start | bytes 32768 | tf_op jit(solution)/shard_map/all_to_all | solution.py:27
  347.7 4.0 %fusion.33 = bf16[2,64,16,128]{3,1,2,0:T(8,128)(2,1)} fusion(f32[2,64,16,128]{3,1,2,0:T(8,128)} %convolution_bitcast_fusion.4, bf16[2,64,16,64]{1,3,2,0:T(8,128)(2,1)S(1)} %copy-done.2, f32[16,2,128,64]{2,1,3,0:T(2,128)S(1)} %fusion.25, f32[2,64,16]{1,2,0:T(8,128)S(1)} %get-tuple-element.33, f32[16,128,64]{1,2,0:T(8,128)S(1)} %fusion.45, ...), kind=kOutput, calls=%fused_computation.41 | convolution fusion | flops 202637312 | bytes 3416192 | tf_op jit(solution)/shard_map/cshe,chde->cshd/dot_general | solution.py:202
  357.4 9.5 %psum.28 = f32[]{:T(128)} all-reduce(f32[]{:T(128)} %multiply_reduce_fusion.2), channel_id=1, replica_groups=mesh['seq_0'=4,'seq_1'=4,'seq_2'=2,'head'=4] {'seq_0'}, use_global_device_ids=true, to_apply=%region_9.10 | all-reduce | flops 1 | bytes 8 | tf_op jit(solution)/shard_map/psum | solution.py:52
  368.1 9.7 %psum.29 = f32[]{:T(128)} all-reduce(f32[]{:T(128)} %psum.28), channel_id=1, replica_groups=mesh['seq_0'=4,'seq_1'=4,'seq_2'=2,'head'=4] {'seq_1'}, use_global_device_ids=true, to_apply=%region_10.11 | all-reduce | flops 1 | bytes 8 | tf_op jit(solution)/shard_map/psum | solution.py:52
  382.4 12.4 %psum.31 = f32[]{:T(128)} all-reduce(f32[]{:T(128)} %psum.30), channel_id=1, replica_groups=mesh['seq_0'=4,'seq_1'=4,'seq_2'=2,'head'=4] {'head'}, use_global_device_ids=true, to_apply=%region_12.13 | all-reduce | flops 1 | bytes 8 | tf_op jit(solution)/shard_map/psum | solution.py:52
  (176 shorter events, 78.3 us)
Async XLA Ops:
  6.3 9.0 %copy-start.7 = (bf16[2,64,16,64]{1,3,2,0:T(8,128)(2,1)}, bf16[2,64,16,64]{1,3,2,0:T(8,128)(2,1)S(1)}, u32[]{:S(2)}) copy-start(bf16[2,64,16,64]{1,3,2,0:T(8,128)(2,1)S(1)} %copy.200) | copy-start | bytes 786436
  15.3 23.5 %copy-start = (f32[2,6,16,128,64]{3,4,1,2,0:T(8,128)}, f32[2,6,16,128,64]{3,4,1,2,0:T(8,128)S(1)}, u32[]{:S(2)}) copy-start(f32[2,6,16,128,64]{3,4,1,2,0:T(8,128)S(1)} %fusion.17) | copy-start | bytes 18874372
  40.7 7.6 %collective-permute-start.9 = (f32[4,16,128,64]{2,3,1,0:T(8,128)}, f32[4,16,128,64]{2,3,1,0:T(8,128)}, u32[]{:S(2)}, u32[]{:S(2)}) collective-permute-start(f32[4,16,128,64]{2,3,1,0:T(8,128)} %slice.109), channel_id=1, source_target_pairs={{0,4},{4,0},{8,12},{12,8},{16,20},{20,16},{24,28},{28,24},{32,36},... | collective-permute-start | bytes 6291464 | tf_op jit(solution)/shard_map/ppermute | solution.py:22
  41.4 7.0 %collective-permute-start.1 = (f32[16]{0:T(128)S(1)}, f32[16]{0:T(128)S(1)}, u32[]{:S(2)}, u32[]{:S(2)}) collective-permute-start(f32[16]{0:T(128)S(1)} %exponential_multiply_fusion.2), channel_id=1, source_target_pairs={{0,4},{4,0},{8,12},{12,8},{16,20},{20,16},{24,28},{28,24},{32,36},... | collective-permute-start | bytes 200 | tf_op jit(solution)/shard_map/ppermute | solution.py:22
  52.0 47.9 %collective-permute-start.10 = (f32[4,16,128,64]{2,3,1,0:T(8,128)}, f32[4,16,128,64]{2,3,1,0:T(8,128)}, u32[]{:S(2)}, u32[]{:S(2)}) collective-permute-start(f32[4,16,128,64]{2,3,1,0:T(8,128)} %add_select_fusion.3), channel_id=1, source_target_pairs={{0,8},{8,0},{4,12},{12,4},{16,24},{24,16},{20,28},{28,20},{32,40},... | collective-permute-start | bytes 6291464 | tf_op jit(solution)/shard_map/ppermute | solution.py:22
  54.5 64.8 %collective-permute-start = (f32[16,128,64]{1,2,0:T(8,128)S(1)}, f32[16,128,64]{1,2,0:T(8,128)}, u32[]{:S(2)}, u32[]{:S(2)}) collective-permute-start(f32[16,128,64]{1,2,0:T(8,128)S(1)} %get-tuple-element.44), channel_id=1, source_target_pairs={{0,4},{4,0},{8,12},{12,8},{16,20},{20,16},{24,28},{28,24},{32,36},... | collective-permute-start | bytes 1572872 | tf_op jit(solution)/shard_map/ppermute | solution.py:22
  59.4 40.4 %collective-permute-start.3 = (f32[16]{0:T(128)S(1)}, f32[16]{0:T(128)S(1)}, u32[]{:S(2)}, u32[]{:S(2)}) collective-permute-start(f32[16]{0:T(128)S(1)} %fusion.102), channel_id=1, source_target_pairs={{0,8},{8,0},{4,12},{12,4},{16,24},{24,16},{20,28},{28,20},{32,40},... | collective-permute-start | bytes 200 | tf_op jit(solution)/shard_map/ppermute | solution.py:22
  104.2 18.0 %copy-start.17 = (bf16[2,64,16,64]{3,2,1,0:T(8,128)(2,1)S(1)}, bf16[2,64,16,64]{3,2,1,0:T(8,128)(2,1)}, u32[]{:S(2)}) copy-start(bf16[2,64,16,64]{3,2,1,0:T(8,128)(2,1)} %reshape.254) | copy-start | bytes 786436
  104.2 92.1 %collective-permute-start.11 = (f32[4,16,128,64]{2,3,1,0:T(8,128)}, f32[4,16,128,64]{2,3,1,0:T(8,128)}, u32[]{:S(2)}, u32[]{:S(2)}) collective-permute-start(f32[4,16,128,64]{2,3,1,0:T(8,128)} %add_select_fusion.2), channel_id=1, source_target_pairs={{0,16},{16,0},{4,20},{20,4},{8,24},{24,8},{12,28},{28,12},{32,48},... | collective-permute-start | bytes 6291464 | tf_op jit(solution)/shard_map/ppermute | solution.py:22
  121.5 57.7 %collective-permute-start.2 = (f32[16,128,64]{1,2,0:T(8,128)}, f32[16,128,64]{1,2,0:T(8,128)}, u32[]{:S(2)}, u32[]{:S(2)}) collective-permute-start(f32[16,128,64]{1,2,0:T(8,128)} %get-tuple-element.27), channel_id=1, source_target_pairs={{0,8},{8,0},{4,12},{12,4},{16,24},{24,16},{20,28},{28,20},{32,40},... | collective-permute-start | bytes 1572872 | tf_op jit(solution)/shard_map/ppermute | solution.py:22
  123.9 61.7 %copy-start.18 = (bf16[16,2,64,64]{2,3,1,0:T(8,128)(2,1)}, bf16[16,2,64,64]{2,3,1,0:T(8,128)(2,1)S(1)}, u32[]{:S(2)}) copy-start(bf16[16,2,64,64]{2,3,1,0:T(8,128)(2,1)S(1)} %get-tuple-element.18) | copy-start | bytes 786436
  123.9 51.8 %collective-permute-start.5 = (f32[16]{0:T(128)S(1)}, f32[16]{0:T(128)S(1)}, u32[]{:S(2)}, u32[]{:S(2)}) collective-permute-start(f32[16]{0:T(128)S(1)} %mul.465), channel_id=1, source_target_pairs={{0,16},{16,0},{4,20},{20,4},{8,24},{24,8},{12,28},{28,12},{32,48},... | collective-permute-start | bytes 200 | tf_op jit(solution)/shard_map/ppermute | solution.py:22
  175.7 3.6 collective-permute-start.7
  181.5 12.4 %collective-permute-start.4 = (f32[16,128,64]{1,2,0:T(8,128)S(1)}, f32[16,128,64]{1,2,0:T(8,128)S(1)}, u32[]{:S(2)}, u32[]{:S(2)}) collective-permute-start(f32[16,128,64]{1,2,0:T(8,128)S(1)} %get-tuple-element.25), channel_id=1, source_target_pairs={{0,16},{16,0},{4,20},{20,4},{8,24},{24,8},{12,28},{28,12},{32,48},... | collective-permute-start | bytes 1572872 | tf_op jit(solution)/shard_map/ppermute | solution.py:22
  193.8 19.1 %slice-start = ((s8[6291456]{0:T(1024)(128)(4,1)}), s8[4194304]{0:T(1024)(128)(4,1)S(1)}, s32[]{:S(2)}) async-start(s8[6291456]{0:T(1024)(128)(4,1)} %bitcast.164), calls=%async_computation.1 | async-start | bytes 8388608
  194.8 18.1 %slice-start.1 = ((s8[6291456]{0:T(1024)(128)(4,1)}), s8[2097152]{0:T(1024)(128)(4,1)S(1)}, s32[]{:S(2)}) async-start(s8[6291456]{0:T(1024)(128)(4,1)} %bitcast.164), calls=%async_computation.2 | async-start | bytes 4194304
  194.8 14.8 %collective-permute-start.6 = (f32[16,128,64]{1,2,0:T(8,128)S(1)}, f32[16,128,64]{1,2,0:T(8,128)S(1)}, u32[]{:S(2)}, u32[]{:S(2)}) collective-permute-start(f32[16,128,64]{1,2,0:T(8,128)S(1)} %get-tuple-element.23), channel_id=1, source_target_pairs={{0,32},{32,0},{4,36},{36,4},{8,40},{40,8},{12,44},{44,12},{16,48},... | collective-permute-start | bytes 1572872 | tf_op jit(solution)/shard_map/ppermute | solution.py:22
  200.7 86.5 %collective-permute-start.12 = (f32[4,16,128,64]{2,3,1,0:T(8,128)}, f32[4,16,128,64]{2,3,1,0:T(8,128)}, u32[]{:S(2)}, u32[]{:S(2)}) collective-permute-start(f32[4,16,128,64]{2,3,1,0:T(8,128)} %add_select_fusion.1), channel_id=1, source_target_pairs={{0,32},{32,0},{4,36},{36,4},{8,40},{40,8},{12,44},{44,12},{16,48},... | collective-permute-start | bytes 6291464 | tf_op jit(solution)/shard_map/ppermute | solution.py:22
  209.8 53.4 %collective-permute-start.8 = (f32[16,128,64]{1,2,0:T(8,128)S(1)}, f32[16,128,64]{1,2,0:T(8,128)S(1)}, u32[]{:S(2)}, u32[]{:S(2)}) collective-permute-start(f32[16,128,64]{1,2,0:T(8,128)S(1)} %add_select_fusion.4), channel_id=1, source_target_pairs={{0,64},{64,0},{4,68},{68,4},{8,72},{72,8},{12,76},{76,12},{16,80},... | collective-permute-start | bytes 1572872 | tf_op jit(solution)/shard_map/ppermute | solution.py:22
  291.7 44.8 %collective-permute-start.13 = (f32[4,16,128,64]{2,3,1,0:T(8,128)}, f32[4,16,128,64]{2,3,1,0:T(8,128)}, u32[]{:S(2)}, u32[]{:S(2)}) collective-permute-start(f32[4,16,128,64]{2,3,1,0:T(8,128)} %add_select_fusion), channel_id=1, source_target_pairs={{0,64},{64,0},{4,68},{68,4},{8,72},{72,8},{12,76},{76,12},{16,80},... | collective-permute-start | bytes 6291464 | tf_op jit(solution)/shard_map/ppermute | solution.py:22
  298.8 8.4 %copy-start.19 = (bf16[16,2,64,64]{2,3,1,0:T(8,128)(2,1)S(1)}, bf16[16,2,64,64]{2,3,1,0:T(8,128)(2,1)}, u32[]{:S(2)}) copy-start(bf16[16,2,64,64]{2,3,1,0:T(8,128)(2,1)} %copy-done.18) | copy-start | bytes 786436
  314.1 24.3 %copy-start.12 = (f32[2,64,16,64]{1,3,2,0:T(8,128)S(1)}, f32[2,64,16,64]{1,3,2,0:T(8,128)}, u32[]{:S(2)}) copy-start(f32[2,64,16,64]{1,3,2,0:T(8,128)} %convolution_bitcast_fusion.2) | copy-start | bytes 1572868
  342.7 12.4 %all-to-all-start = ((f32[32,1,16]{2,1,0:T(1,128)}), f32[32,1,16]{2,1,0:T(1,128)S(1)}, u32[]{:S(2)}, u32[]{:S(2)}) async-start(f32[32,1,16]{2,1,0:T(1,128)} %broadcast_in_dim.166), calls=%async_computation | async-start | bytes 32768 | tf_op jit(solution)/shard_map/all_to_all | solution.py:27
  347.7 19.2 %copy-start.20 = (bf16[2,64,16,128]{3,2,1,0:T(8,128)(2,1)S(1)}, bf16[2,64,16,128]{3,2,1,0:T(8,128)(2,1)}, u32[]{:S(2)}) copy-start(bf16[2,64,16,128]{3,2,1,0:T(8,128)(2,1)} %copy.203) | copy-start | bytes 1572868
  (16 other events, 79.1 us)
where the time goes:
time: 404 us; the launch traced here: 397 us
  waiting for transfers between devices  166 us (41%)
  matrix products  79.7 us (20%)
  local copies, waits for them, and re-layouts  39.9 us (10%)
  other arithmetic  37 us (9%)
  starting transfers between devices  36.5 us (9%)
  blocking collectives  34.8 us (9%)
    ppermute x14, waiting for transfers between devices, from_partner(): return lax.ppermute(block, axis, route)  162 us
    psum x4, blocking collectives, one_axis_at_a_time(): shard = lax.psum(shard, axis)  34.8 us
    ppermute x14, starting transfers between devices, from_partner(): return lax.ppermute(block, axis, route)  31.5 us
    dot_general x1, matrix products, shards(): jnp.einsum('hc,clhde->lhde', lead_decay, back_local, precision=exact_mode)  23.4 us
    select_n x4, other arithmetic, shards(): jnp.where(upper, other_state + other_decay[None, :, None, None] * block_s...  16.8 us
    dot_general x1, matrix products, shards(): jnp.einsum('hts,lts,tlhde->shde', between, level_hot, back_local, precisi...  13 us
    another operation x2, local copies, waits for them, and re-layouts, shards(): jnp.stack(incoming)[None]  12.4 us
    dot_general x1, matrix products, shards(): jnp.einsum('hjs,ljs,shde->jlhde', between, level_hot, span_state, precisi...  10.6 us
  transfers between devices with their start and end apart: 15, of which 8 were waited for; matrix products, arithmetic and copies ran while one was open for 24% of the time, Pallas kernels for 0%

commit v1 on v0

v1 whole, which is shorter than its diff:
```python
import functools

import jax
import jax.numpy as jnp
from jax import lax
from jax.experimental import pallas as pl
from jax.experimental.pallas import tpu as pltpu
from jax.sharding import Mesh
from jax.sharding import PartitionSpec as P

SEQ = ("seq_0", "seq_1", "seq_2")
MESH = pl.DeviceIdType.MESH
F32 = jnp.float32
BF16 = jnp.bfloat16
NEG = -1e30

NN = (((1,), (0,)), ((), ()))
NT = (((1,), (1,)), ((), ()))
TN = (((0,), (0,)), ((), ()))


def dot(a, b, dims):
    return lax.dot_general(a, b, dims, preferred_element_type=F32)


def split(a):
    hi = a.astype(BF16)
    return hi, (a - hi.astype(F32)).astype(BF16)


def prefix(a, lane):
    shift = 1
    while shift < a.shape[1]:
        a = a + jnp.where(lane >= shift, pltpu.roll(a, shift, 1), 0.0)
        shift *= 2
    return a


def suffix(a, lane):
    size = a.shape[1]
    shift = 1
    while shift < size:
        a = a + jnp.where(lane < size - shift, pltpu.roll(a, size - shift, 1), 0.0)
        shift *= 2
    return a


def kernel(
    q_in, k_in, v_in, g_in, lg_in, lw_in, ds_in,
    gq_out, gk_out, gv_out, glw_out, glg_out,
    sq, sk, sv, sg, ss, rq, rk, rv, rg, rs,
    qb, kb, vb, gb, vt, gt,
    gates, doc, cum, fs, de, wts, cm, bias, pt, rt,
    gq, gk, gv, gvt, glw, drift, small,
    ys, yr, zs, zr, xs, xr, ein, xin,
    bq, bk, bv, bs,
    a_buf, b_buf,
    in_send, in_recv, y1_send, y1_recv, y2_send, y2_recv, x_send, x_recv,
    out_send, out_recv, last_send, last_recv, a_send, a_recv, b_send, b_recv,
):
    x, y, c, z = (lax.axis_index(n) for n in ("seq_0", "seq_1", "seq_2", "head"))
    other = 1 - c
    chip = x * 4 + y
    group = z * 2 + c

    def remote(src, dst, send, recv, **to):
        return pltpu.make_async_remote_copy(
            src_ref=src, dst_ref=dst, send_sem=send, recv_sem=recv,
            device_id=to, device_id_type=MESH,
        )

    barrier = pltpu.get_barrier_semaphore()
    for step in range(1, 16):
        peer = (chip + step) % 16
        pl.semaphore_signal(
            barrier, inc=1, device_id={"seq_0": peer // 4, "seq_1": peer % 4}, device_id_type=MESH
        )
    for step in range(1, 8):
        peer = (group + step) % 8
        pl.semaphore_signal(
            barrier, inc=1, device_id={"head": peer // 2, "seq_2": peer % 2}, device_id_type=MESH
        )

    q_cols = pl.ds(pl.multiple_of(other * 1024, 1024), 1024)
    v_cols = pl.ds(pl.multiple_of(other * 512, 512), 512)
    own_q = pl.ds(pl.multiple_of(c * 1024, 1024), 1024)
    own_v = pl.ds(pl.multiple_of(c * 512, 512), 512)
    own_rows = pl.ds(pl.multiple_of(c * 128, 128), 128)
    other_rows = pl.ds(pl.multiple_of(other * 128, 128), 128)
    own_heads = pl.ds(pl.multiple_of(c * 8, 8), 8)
    other_heads = pl.ds(pl.multiple_of(other * 8, 8), 8)
    ds_row = jnp.broadcast_to(ds_in[...].astype(F32), (8, 128))
    ss[0:8, :] = lg_in[other_heads, :]
    for level in range(6):
        ss[8 + 8 * level : 16 + 8 * level, :] = lw_in[level, other_heads, :]
    ss[56:64, :] = ds_row
    sk[...] = k_in[:, q_cols].astype(F32)
    sv[...] = v_in[:, v_cols].astype(F32)
    sg[...] = g_in[:, v_cols].astype(F32)
    sq[...] = q_in[:, q_cols].astype(F32)

    pl.semaphore_wait(barrier, 22)
    swaps = [
        remote(src, dst, in_send.at[n], in_recv.at[n], seq_2=other)
        for n, (src, dst) in enumerate(((ss, rs), (sk, rk), (sv, rv), (sg, rg), (sq, rq)))
    ]
    for swap in swaps:
        swap.start()

    kb[own_rows, :] = k_in[:, own_q]
    vb[own_rows, :] = v_in[:, own_v]
    gb[own_rows, :] = g_in[:, own_v]
    qb[own_rows, :] = q_in[:, own_q]
    gates[:, own_rows] = lg_in[own_heads, :]
    for level in range(6):
        wts[level, :, own_rows] = lw_in[level, own_heads, :]
    doc[:, own_rows] = ds_row
    ein[...] = jnp.zeros_like(ein)
    xin[...] = jnp.zeros_like(xin)
    pt[128:256, 0:128] = jnp.zeros((128, 128), BF16)
    rt[128:256, 0:128] = jnp.zeros((128, 128), BF16)

    zero_slab = jnp.zeros((128, 128), F32)
    for level, absent in ((0, y % 2 == 0), (1, y < 2), (2, x == 0)):

        @pl.when(absent)
        def _():
            for pair in range(4):
                zr[pair, level] = zero_slab

    swaps[0].wait_recv()
    gates[:, other_rows] = rs[0:8, :]
    for level in range(6):
        wts[level, :, other_rows] = rs[8 + 8 * level : 16 + 8 * level, :]
    doc[:, other_rows] = rs[56:64, :]
    lane = lax.broadcasted_iota(jnp.int32, (8, 256), 1)
    cum_now = prefix(gates[...], lane)
    reset = prefix(doc[...], lane)
    total = cum_now[:, 255:256]
    reset_total = reset[:, 255:256]
    cum[...] = cum_now
    fs[...] = jnp.where(reset == 0.0, jnp.exp(cum_now), 0.0)
    de[...] = jnp.where(reset == reset_total, jnp.exp(total - cum_now), 0.0)
    decay = jnp.broadcast_to(jnp.where(reset_total == 0.0, jnp.exp(total), 0.0), (8, 128))
    small[...] = decay
    columns = jnp.transpose(
        jnp.concatenate([cum_now, reset, jnp.zeros((112, 256), F32)], axis=0)
    )
    for head in range(8):
        cm[head] = jnp.broadcast_to(columns[:, head : head + 1], (256, 128))
    reset_col = jnp.broadcast_to(columns[:, 8:9], (256, 128))
    for half in range(2):
        reset_row = jnp.broadcast_to(reset[0:1, 128 * half : 128 * half + 128], (256, 128))
        s_pos = lax.broadcasted_iota(jnp.int32, (256, 128), 0)
        t_pos = lax.broadcasted_iota(jnp.int32, (256, 128), 1) + 128 * half
        bias[:, 128 * half : 128 * half + 128] = jnp.where(
            (t_pos >= s_pos) & (reset_col == reset_row), 0.0, NEG
        )

    swaps[1].wait_recv()
    kb[other_rows, :] = rk[...].astype(BF16)
    swaps[2].wait_recv()
    vb[other_rows, :] = rv[...].astype(BF16)
    swaps[3].wait_recv()
    gb[other_rows, :] = rg[...].astype(BF16)
    swaps[4].wait_recv()
    qb[other_rows, :] = rq[...].astype(BF16)

    def head_cols(pair, i):
        return pl.ds(pl.multiple_of(pair * 256 + i * 128, 128), 128)

    def pair_cols(pair):
        return pl.ds(pl.multiple_of(pair * 128, 128), 128)

    def sent(kind, at_y):
        return (True, x > 0, at_y % 2 == 1, at_y >= 2)[kind]

    def y1_copy(pair, kind, at_y):
        rows = 136 if kind == 0 else 128
        return remote(
            ys.at[pair, kind, pl.ds(0, rows)], yr.at[at_y, kind, pl.ds(0, rows)],
            y1_send.at[pair, kind], y1_recv.at[at_y, kind], seq_1=pair,
        )

    def states(pair):
        vt[pair] = jnp.transpose(vb[:, pair_cols(pair)].astype(F32))
        gt[pair] = jnp.transpose(gb[:, pair_cols(pair)].astype(F32))
        for i in range(2):
            head = pl.ds(pair * 2 + i, 1)
            rows = pl.ds(64 * i, 64)
            gate = fs[head, :]
            value_hi, value_lo = split(vt[pair, rows] * de[head, :])
            parts = [split(gt[pair, rows] * (gate * wts[level, head, :])) for level in (5, 3, 4)]
            state = dot(
                jnp.concatenate([value_hi, value_lo], axis=0), kb[:, head_cols(pair, i)], NN
            )
            back = dot(
                jnp.concatenate([p[0] for p in parts] + [p[1] for p in parts], axis=0),
                qb[:, head_cols(pair, i)], NN,
            )
            slabs = [state[0:64] + state[64:128]] + [
                back[64 * n : 64 * n + 64] + back[192 + 64 * n : 256 + 64 * n] for n in range(3)
            ]
            row = small[head, :]

            @pl.when(pair == y)
            def _():
                for kind in range(4):
                    yr[y, kind, rows] = slabs[kind]
                yr[y, 0, 128 + i : 129 + i] = row

            @pl.when(pair != y)
            def _():
                for kind in range(4):
                    ys[pair, kind, rows] = slabs[kind]
                ys[pair, 0, 128 + i : 129 + i] = row

        for kind in range(4):

            @pl.when((pair != y) & sent(kind, y))
            def _():
                y1_copy(pair, kind, y).start()

    def intra(pair):
        for i in range(2):
            number = pair * 2 + i
            head = pl.ds(number, 1)
            rows = pl.ds(64 * i, 64)
            query = qb[:, head_cols(pair, i)]
            key = kb[:, head_cols(pair, i)]
            grad = gb[:, pair_cols(pair)]
            value = vb[:, pair_cols(pair)]
            mine = lax.broadcasted_iota(jnp.int32, (64, 128), 1) // 64 == i
            weight = [wts[level, head, :] for level in range(3)]
            span = lax.broadcasted_iota(jnp.int32, (1, 256), 1) // 64
            cum_row = cum[head, :]
            level_rows = [jnp.zeros((1, 256), F32) for level in range(3)]
            drift_row = jnp.zeros((1, 256), F32)
            for b in range(4):
                low = 0 if b < 2 else 128
                blk = slice(64 * b, 64 * b + 64)
                score = dot(key[blk], query[low:256], NT)
                pair_dot = dot(
                    jnp.where(mine, value[blk], jnp.zeros((64, 128), BF16)), grad[low:256], NT
                )
                col = cm[number, blk, :]
                if low == 0:
                    col = jnp.concatenate([col, col], axis=1)
                decayed = jnp.exp((cum_row[:, low:256] - col) + bias[blk, low:256])
                at = span[:, low:256]
                near = (at == b).astype(jnp.int32), ((at ^ 1) == b).astype(jnp.int32)
                mix = jnp.where(
                    near[0] == 1, weight[0][:, low:256],
                    jnp.where(near[1] == 1, weight[1][:, low:256], weight[2][:, low:256]),
                )
                scored = decayed * score
                joint = jnp.sum(scored * pair_dot, axis=0, keepdims=True)
                prob = (scored * mix).astype(BF16)
                pt[blk, low:256] = prob
                rt[blk, low:256] = (decayed * mix * pair_dot).astype(BF16)
                drifted = jnp.sum(prob.astype(F32) * pair_dot, axis=0, keepdims=True)
                if low:
                    pad = jnp.zeros((1, 128), F32)
                    joint = jnp.concatenate([pad, joint], axis=1)
                    drifted = jnp.concatenate([pad, drifted], axis=1)
                drift_row = drift_row + drifted
                level_rows[0] = level_rows[0] + jnp.where(span == b, joint, 0.0)
                level_rows[1] = level_rows[1] + jnp.where((span ^ 1) == b, joint, 0.0)
                level_rows[2] = level_rows[2] + jnp.where(
                    (span != b) & ((span ^ 1) != b), joint, 0.0
                )
            for level in range(3):
                glw[level, head, :] = level_rows[level]
            drift[head, :] = drift_row
            gvt[pair, rows] = dot(gt[pair, rows].astype(BF16), pt[...], NT)
            gk[:, head_cols(pair, i)] = dot(rt[...], query, NN)
            gq[:, head_cols(pair, i)] = dot(rt[...], key, TN)

    def y2_copy(to_y, kind, src):
        return remote(
            src, zr.at[y, kind], y2_send.at[to_y, kind], y2_recv.at[y, kind], seq_1=to_y
        )

    def y2_source(to_y, kind):
        if kind == 0:
            return yr.at[to_y - 1, 0, pl.ds(0, 128)]
        return zs.at[to_y, kind]

    def hand_back(to_y, kind):
        def go():
            @pl.when(to_y != y)
            def _():
                y2_copy(to_y, kind, y2_source(to_y, kind)).start()

            @pl.when(to_y == y)
            def _():
                zr[y, kind] = y2_source(to_y, kind)[...]

        if kind == 2:
            pl.when(x > 0)(go)
        else:
            go()

    def y1_wait(kind):
        for at_y in range(4):
            here = sent(kind, at_y)
            if here is False:
                continue

            @pl.when((y != at_y) & here)
            def _():
                y1_copy(y, kind, at_y).wait_recv()

    def x_copy(to_x, kind):
        return remote(xs.at[kind], xr.at[x], x_send.at[to_x], x_recv.at[x], seq_0=to_x)

    def combine_first():
        y1_wait(0)
        y1_wait(1)
        for i in range(2):
            rows = slice(64 * i, 64 * i + 64)
            dec = [yr[n, 0, 128 + i : 129 + i] for n in range(4)]
            both = dec[1] * yr[0, 0, rows] + yr[1, 0, rows]
            zs[2, 1, rows] = both
            after = dec[2] * both
            zs[3, 1, rows] = after
            xs[0, rows] = dec[3] * (after + yr[2, 0, rows]) + yr[3, 0, rows]
            all_decay = dec[0] * dec[1] * (dec[2] * dec[3])
            xs[0, 128 + i : 129 + i] = all_decay
            xs[1, 128 + i : 129 + i] = all_decay

            @pl.when(x > 0)
            def _():
                back = yr[2, 1, rows] + dec[2] * yr[3, 1, rows]
                back = yr[1, 1, rows] + dec[1] * back
                xs[1, rows] = yr[0, 1, rows] + dec[0] * back

        for to_x in range(4):

            @pl.when(to_x > x)
            def _():
                x_copy(to_x, 0).start()

            @pl.when(to_x < x)
            def _():
                x_copy(to_x, 1).start()

        hand_back(1, 0)
        hand_back(3, 0)
        hand_back(2, 1)
        hand_back(3, 1)

    def combine_second():
        y1_wait(2)
        y1_wait(3)

        def take(at_x, acc):
            remote(
                xs.at[0], xr.at[at_x], x_send.at[at_x], x_recv.at[at_x], seq_0=at_x
            ).wait_recv()
            for i in range(2):
                rows = slice(64 * i, 64 * i + 64)
                acc[rows] = xr[at_x, 128 + i : 129 + i] * acc[rows] + xr[at_x, rows]

        for at_x in range(4):
            pl.when(at_x < x)(functools.partial(take, at_x, ein))
        for at_x in range(3, -1, -1):
            pl.when(at_x > x)(functools.partial(take, at_x, xin))
        for i in range(2):
            rows = slice(64 * i, 64 * i + 64)
            dec = [yr[n, 0, 128 + i : 129 + i] for n in range(4)]
            into = ein[rows]
            for at_y in range(4):
                zs[at_y, 2, rows] = into
                into = dec[at_y] * into
            late = xin[rows]
            zs[3, 3, rows] = late
            late = dec[3] * late
            zs[2, 3, rows] = late + yr[3, 2, rows]
            late = dec[2] * late + (yr[2, 3, rows] + dec[2] * yr[3, 3, rows])
            zs[1, 3, rows] = late
            zs[0, 3, rows] = dec[1] * late + yr[1, 2, rows]
        for at_y in range(4):
            hand_back(at_y, 2)
            hand_back(at_y, 3)

    def back_copy(pair, kind):
        if kind == 2:
            cols, src, dst = pair_cols(pair), gv, bv
        else:
            cols = pl.ds(pl.multiple_of(pair * 256, 256), 256)
            src, dst = ((gq, bq), (gk, bk))[kind]
        return remote(
            src.at[other_rows, cols], dst.at[:, cols],
            out_send.at[pair, kind], out_recv.at[pair, kind], seq_2=other,
        )

    def cross(pair):
        for kind in range(4):
            here = (y % 2 == 1, y >= 2, x > 0, True)[kind]

            @pl.when((pair != y) & here)
            def _():
                remote(
                    zs.at[0, kind], zr.at[pair, kind], y2_send.at[0, kind],
                    y2_recv.at[pair, kind], seq_1=pair,
                ).wait_recv()

        for i in range(2):
            number = pair * 2 + i
            head = pl.ds(number, 1)
            rows = pl.ds(64 * i, 64)
            query = qb[:, head_cols(pair, i)]
            key = kb[:, head_cols(pair, i)]
            grad = gt[pair, rows]
            value = vt[pair, rows]
            gate = fs[head, :]
            end = de[head, :]
            weight = [wts[level, head, :] for level in (3, 4, 5)]
            enter = jnp.concatenate([zr[pair, n, rows] for n in range(3)], axis=0)
            enter_hi, enter_lo = split(enter)
            mixed = dot(jnp.concatenate([enter_hi, enter_lo], axis=0), query, NT)
            drift_row = drift[head, :]
            for n in range(3):
                state_row = mixed[64 * n : 64 * n + 64] + mixed[192 + 64 * n : 256 + 64 * n]
                level_row = gate * jnp.sum(state_row * grad, axis=0, keepdims=True)
                glw[3 + n, head, :] = level_row
                drift_row = drift_row + weight[n] * level_row
            weighted_hi, weighted_lo = split(
                jnp.concatenate([grad * (gate * weight[n]) for n in range(3)], axis=0)
            )
            gq[:, head_cols(pair, i)] = gq[:, head_cols(pair, i)] + dot(
                jnp.concatenate([weighted_hi, weighted_lo, weighted_hi], axis=0),
                jnp.concatenate([enter_hi, enter_hi, enter_lo], axis=0), TN,
            )
            leave_hi, leave_lo = split(zr[pair, 3, rows])
            left = dot(jnp.concatenate([leave_hi, leave_lo], axis=0), key, NT)
            value_grad = gvt[pair, rows] + end * (left[0:64] + left[64:128])
            gvt[pair, rows] = value_grad
            drift[head, :] = drift_row - jnp.sum(value * value_grad, axis=0, keepdims=True)
            ended_hi, ended_lo = split(value * end)
            gk[:, head_cols(pair, i)] = gk[:, head_cols(pair, i)] + dot(
                jnp.concatenate([ended_hi, ended_lo, ended_hi], axis=0),
                jnp.concatenate([leave_hi, leave_hi, leave_lo], axis=0), TN,
            )
        gv[:, pair_cols(pair)] = jnp.transpose(gvt[pair])
        for kind in range(3):
            back_copy(pair, kind).start()
        wide = pl.ds(pl.multiple_of(pair * 256, 256), 256)
        out_wide = pl.ds(pl.multiple_of(c * 1024 + pair * 256, 256), 256)
        out_narrow = pl.ds(pl.multiple_of(c * 512 + pair * 128, 128), 128)
        gq_out[:, out_wide] = gq[own_rows, wide].astype(BF16)
        gk_out[:, out_wide] = gk[own_rows, wide].astype(BF16)
        gv_out[:, out_narrow] = gv[own_rows, pair_cols(pair)].astype(BF16)

    def loop(low, high, body):
        def step(n, carry):
            body(n)
            return carry

        lax.fori_loop(low, high, step, 0)

    loop(0, 4, states)
    loop(0, 2, intra)
    combine_first()
    loop(2, 4, intra)
    combine_second()
    loop(0, 4, cross)

    lane = lax.broadcasted_iota(jnp.int32, (8, 256), 1)
    tail = suffix(drift[...], lane)
    drift[...] = tail
    bs_out = remote(small.at[:, :], bs.at[pl.ds(48, 8), :], last_send.at[1], last_recv.at[1], seq_2=other)
    tile = lax.broadcasted_iota(jnp.int32, (8, 128), 1)
    head_total = jnp.broadcast_to(tail[:, 0:1], (8, 128))
    head_square = jnp.broadcast_to(jnp.sum(tail * tail, axis=1, keepdims=True), (8, 128))
    head_sum = jnp.broadcast_to(jnp.sum(tail, axis=1, keepdims=True), (8, 128))
    a_buf[chip] = jnp.where(tile == 0, head_total, jnp.where(tile == 1, head_square, head_sum))

    def a_copy(step):
        peer = (chip + step) % 16
        return remote(
            a_buf.at[chip], a_buf.at[chip], a_send.at[peer], a_recv.at[chip],
            seq_0=peer // 4, seq_1=peer % 4,
        )

    for step in range(1, 16):
        a_copy(step).start()
    small[...] = drift[:, other_rows]
    for level in range(6):
        ss_rows = slice(8 * level, 8 * level + 8)
        ys[y, 1, ss_rows] = glw[level, :, other_rows]
    glw_copy = remote(
        ys.at[y, 1, pl.ds(0, 48)], bs.at[pl.ds(0, 48), :], last_send.at[0], last_recv.at[0],
        seq_2=other,
    )
    glw_copy.start()
    bs_out.start()
    for level in range(6):
        glw_out[level, own_heads, :] = glw[level, :, own_rows]

    for pair in range(4):
        for kind in range(3):
            back_copy(pair, kind).wait_recv()
    other_q = pl.ds(pl.multiple_of(other * 1024, 1024), 1024)
    other_v = pl.ds(pl.multiple_of(other * 512, 512), 512)
    gq_out[:, other_q] = bq[...].astype(BF16)
    gk_out[:, other_q] = bk[...].astype(BF16)
    gv_out[:, other_v] = bv[...].astype(BF16)
    glw_copy.wait_recv()
    for level in range(6):
        glw_out[level, other_heads, :] = bs[8 * level : 8 * level + 8, :]

    for step in range(1, 16):
        peer = (chip + step) % 16
        remote(
            a_buf.at[chip], a_buf.at[peer], a_send.at[peer], a_recv.at[peer],
            seq_0=peer // 4, seq_1=peer % 4,
        ).wait_recv()
    run = jnp.zeros((8, 1), F32)
    later = jnp.zeros((8, 1), F32)
    squares = jnp.zeros((8, 1), F32)
    for at in range(15, -1, -1):
        now = a_buf[at]
        later = later + run * (chip == at).astype(F32)
        squares = squares + now[:, 1:2] + run * (2.0 * now[:, 2:3] + 256.0 * run)
        run = run + now[:, 0:1]
    whole = jnp.broadcast_to(jnp.sum(squares, axis=0, keepdims=True), (8, 128))
    b_buf[group] = jnp.where(tile < 64, jnp.broadcast_to(later, (8, 128)), whole)

    def b_peer(step):
        peer = (group + step) % 8
        return peer, {"head": peer // 2, "seq_2": peer % 2}

    for step in range(1, 8):
        peer, to = b_peer(step)
        remote(
            b_buf.at[group], b_buf.at[group], b_send.at[peer], b_recv.at[group], **to
        ).start()
    for step in range(1, 8):
        peer, to = b_peer(step)
        remote(
            b_buf.at[group], b_buf.at[peer], b_send.at[peer], b_recv.at[peer], **to
        ).wait_recv()
    total_square = jnp.zeros((8, 128), F32)
    for at in range(8):
        total_square = total_square + b_buf[at]
    factor = jnp.minimum(1.0, lax.rsqrt(total_square[:, 64:65] / (64 * 4096) + 1e-06))
    glg_out[own_heads, :] = (drift[:, own_rows] + later) * factor
    bs_out.wait_recv()
    glg_out[other_heads, :] = (bs[48:56, :] + b_buf[z * 2 + other][:, 0:1]) * factor

    for swap in swaps:
        swap.wait_send()
    for pair in range(4):
        for kind in range(4):

            @pl.when((y != pair) & sent(kind, y))
            def _():
                y1_copy(pair, kind, y).wait_send()

            back = (pair % 2 == 1, pair >= 2, x > 0, True)[kind]
            if back is not False:

                @pl.when((y != pair) & back)
                def _():
                    y2_copy(pair, kind, y2_source(pair, kind)).wait_send()

        @pl.when(pair != x)
        def _():
            x_copy(pair, 0).wait_send()

        for kind in range(3):
            back_copy(pair, kind).wait_send()
    glw_copy.wait_send()
    bs_out.wait_send()
    for step in range(1, 16):
        a_copy(step).wait_send()
    for step in range(1, 8):
        peer, to = b_peer(step)
        remote(
            b_buf.at[group], b_buf.at[group], b_send.at[peer], b_recv.at[group], **to
        ).wait_send()


def shards(queries, keys, values, out_grad, log_gate, level_weight, doc_start):
    vmem = pl.BlockSpec(memory_space=pltpu.VMEM)
    scratch = (
        [(128, 1024), (128, 1024), (128, 512), (128, 512), (64, 128)] * 2
    )
    scratch = [pltpu.VMEM(s, F32) for s in scratch]
    scratch += [pltpu.VMEM(s, BF16) for s in ((256, 1024), (256, 1024), (256, 512), (256, 512))]
    scratch += [pltpu.VMEM((4, 128, 256), F32)] * 2
    scratch += [pltpu.VMEM((8, 256), F32)] * 5
    scratch += [pltpu.VMEM((6, 8, 256), F32), pltpu.VMEM((8, 256, 128), F32)]
    scratch += [pltpu.VMEM((256, 256), F32), pltpu.VMEM((256, 256), BF16), pltpu.VMEM((256, 256), BF16)]
    scratch += [pltpu.VMEM((256, 1024), F32), pltpu.VMEM((256, 1024), F32), pltpu.VMEM((256, 512), F32)]
    scratch += [pltpu.VMEM((4, 128, 256), F32), pltpu.VMEM((6, 8, 256), F32)]
    scratch += [pltpu.VMEM((8, 256), F32), pltpu.VMEM((8, 128), F32)]
    scratch += [pltpu.VMEM((4, 4, 136, 128), F32)] * 2 + [pltpu.VMEM((4, 4, 128, 128), F32)] * 2
    scratch += [pltpu.VMEM((2, 136, 128), F32), pltpu.VMEM((4, 136, 128), F32)]
    scratch += [pltpu.VMEM((128, 128), F32)] * 2
    scratch += [pltpu.VMEM((128, 1024), F32), pltpu.VMEM((128, 1024), F32), pltpu.VMEM((128, 512), F32)]
    scratch += [pltpu.VMEM((56, 128), F32)]
    scratch += [pltpu.VMEM((16, 8, 128), F32), pltpu.VMEM((8, 8, 128), F32)]
    sems = [(5,), (5,), (4, 4), (4, 4), (4, 4), (4, 4), (4,), (4,), (4, 3), (4, 3), (2,), (2,)]
    sems += [(16,), (16,), (8,), (8,)]
    scratch += [pltpu.SemaphoreType.DMA(s) for s in sems]
    return pl.pallas_call(
        kernel,
        out_shape=(
            jax.ShapeDtypeStruct(queries.shape, BF16),
            jax.ShapeDtypeStruct(keys.shape, BF16),
            jax.ShapeDtypeStruct(values.shape, BF16),
            jax.ShapeDtypeStruct(level_weight.shape, F32),
            jax.ShapeDtypeStruct(log_gate.shape, F32),
        ),
        in_specs=[vmem] * 7,
        out_specs=[vmem] * 5,
        scratch_shapes=scratch,
        compiler_params=pltpu.CompilerParams(
            collective_id=0, has_side_effects=True, vmem_limit_bytes=56 * 2**20
        ),
    )(queries, keys, values, out_grad, log_gate, level_weight, doc_start.reshape(1, -1))


def solution(mesh):
    finer = Mesh(
        mesh.devices.reshape(4, 4, 2, mesh.shape["head"]), ("seq_0", "seq_1", "seq_2", "head")
    )
    wide = P(SEQ, "head")
    return jax.shard_map(
        shards,
        mesh=finer,
        in_specs=(wide, wide, wide, wide, P("head", SEQ), P(None, "head", SEQ), P(SEQ)),
        out_specs=(wide, wide, wide, P(None, "head", SEQ), P("head", SEQ)),
        check_vma=False,
    )
```

time: 404 us -> 58.6 us (0.15)
  the two profiles are of different devices: /device:TPU:0 before, /device:TPU:1 now
where the time goes in v1:
time: 58.6 us; the launch traced here: 58.3 us
  Pallas kernels  52.5 us (90%)
  local copies, waits for them, and re-layouts  5.13 us (9%)
  between operations  0.66 us (1%)
    pallas_call x1, Pallas kernels, shards(): pl.pallas_call(kernel, out_shape=(jax.ShapeDtypeStruct(queries.shape, BF1...  52.5 us
    unnamed x13, local copies, waits for them, and re-layouts  5.13 us

profile of v1, /device:TPU:1, one launch (start us, length us, event | category | flops | bytes accessed | tf_op | source)
XLA Modules:
  0.0 58.3 jit_solution(2541291208279065343)
XLA Ops:
  0.6 52.5 %shard_map.110 = (bf16[128,2048]{1,0:T(8,128)(2,1)}, bf16[128,2048]{1,0:T(8,128)(2,1)}, bf16[128,1024]{1,0:T(8,128)(2,1)}, f32[6,16,128]{2,1,0:T(8,128)}, f32[16,128]{1,0:T(8,128)}) custom-call(bf16[128,2048]{1,0:T(8,128)(2,1)} %q_in.1, bf16[128,2048]{1,0:T(8,128)(2,1)} %k_in.1, bf16[128,1024]{1,0:T(8,128)(2,1)} %v_in.1, bf16[128,1024]{1,0:T(8,128)(2,1)} %g_in.1, ...), custom_call_target="tpu_custom_call" | custom-call | tf_op jit(solution)/shard_map/pallas_call | solution.py:609
  53.2 0.0 copy-start
  53.2 1.9 %copy.17 = bf16[128,2048]{1,0:T(8,128)(2,1)} copy(bf16[128,2048]{1,0:T(8,128)(2,1)} %get-tuple-element.10) | data formatting | bytes 1048576
  55.1 0.0 copy-done
  55.1 0.0 copy-start.1
  55.1 0.8 %copy.18 = bf16[128,2048]{1,0:T(8,128)(2,1)} copy(bf16[128,2048]{1,0:T(8,128)(2,1)S(1)} %copy-done) | data formatting | bytes 1048576
  55.9 0.3 copy-done.1
  56.2 0.0 copy-start.2
  56.2 0.7 %copy.19 = bf16[128,1024]{1,0:T(8,128)(2,1)} copy(bf16[128,1024]{1,0:T(8,128)(2,1)S(1)} %copy-done.1) | data formatting | bytes 524288
  56.9 0.1 copy-done.2
  57.0 0.0 copy-start.3
  57.0 0.6 %copy.20 = f32[6,16,128]{2,1,0:T(8,128)} copy(f32[6,16,128]{2,1,0:T(8,128)S(1)} %copy-done.2) | data formatting | bytes 98304
  57.7 0.1 copy-done.3
  57.7 0.6 %copy.21 = f32[16,128]{1,0:T(8,128)} copy(f32[16,128]{1,0:T(8,128)S(1)} %copy-done.3) | data formatting | bytes 16384
Async XLA Ops:
  53.2 2.0 %copy-start = (bf16[128,2048]{1,0:T(8,128)(2,1)S(1)}, bf16[128,2048]{1,0:T(8,128)(2,1)}, u32[]{:S(2)}) copy-start(bf16[128,2048]{1,0:T(8,128)(2,1)} %get-tuple-element.11) | copy-start | bytes 1572868
  55.1 1.1 %copy-start.1 = (bf16[128,1024]{1,0:T(8,128)(2,1)S(1)}, bf16[128,1024]{1,0:T(8,128)(2,1)}, u32[]{:S(2)}) copy-start(bf16[128,1024]{1,0:T(8,128)(2,1)} %get-tuple-element.12) | copy-start | bytes 786436
  56.2 0.8 %copy-start.2 = (f32[6,16,128]{2,1,0:T(8,128)S(1)}, f32[6,16,128]{2,1,0:T(8,128)}, u32[]{:S(2)}) copy-start(f32[6,16,128]{2,1,0:T(8,128)} %get-tuple-element.13) | copy-start | bytes 147460
  57.0 0.7 %copy-start.3 = (f32[16,128]{1,0:T(8,128)S(1)}, f32[16,128]{1,0:T(8,128)}, u32[]{:S(2)}) copy-start(f32[16,128]{1,0:T(8,128)} %get-tuple-element.14) | copy-start | bytes 24580

commit v2 on v1

--- a/solution.py
+++ b/solution.py
@@ -46,8 +46,10 @@
 
 
 def kernel(
+    q_hbm, k_hbm, v_hbm, g_hbm, lg_hbm, lw_hbm, ds_hbm,
+    gq_hbm, gk_hbm, gv_hbm, glw_hbm, glg_hbm,
     q_in, k_in, v_in, g_in, lg_in, lw_in, ds_in,
-    gq_out, gk_out, gv_out, glw_out, glg_out,
+    gq_out, gk_out, gv_out, glw_out, glg_out, load_sem, store_sem,
     sq, sk, sv, sg, ss, rq, rk, rv, rg, rs,
     qb, kb, vb, gb, vt, gt,
     gates, doc, cum, fs, de, wts, cm, bias, pt, rt,
@@ -69,6 +71,16 @@
             device_id=to, device_id_type=MESH,
         )
 
+    loads = [
+        pltpu.make_async_copy(src, dst, load_sem.at[n])
+        for n, (src, dst) in enumerate((
+            (ds_hbm, ds_in), (lg_hbm, lg_in), (lw_hbm, lw_in), (k_hbm, k_in),
+            (v_hbm, v_in), (g_hbm, g_in), (q_hbm, q_in),
+        ))
+    ]
+    for load in loads:
+        load.start()
+
     barrier = pltpu.get_barrier_semaphore()
     for step in range(1, 16):
         peer = (chip + step) % 16
@@ -89,14 +101,20 @@
     other_rows = pl.ds(pl.multiple_of(other * 128, 128), 128)
     own_heads = pl.ds(pl.multiple_of(c * 8, 8), 8)
     other_heads = pl.ds(pl.multiple_of(other * 8, 8), 8)
+    for load in loads[:3]:
+        load.wait()
     ds_row = jnp.broadcast_to(ds_in[...].astype(F32), (8, 128))
     ss[0:8, :] = lg_in[other_heads, :]
     for level in range(6):
         ss[8 + 8 * level : 16 + 8 * level, :] = lw_in[level, other_heads, :]
     ss[56:64, :] = ds_row
+    loads[3].wait()
     sk[...] = k_in[:, q_cols].astype(F32)
+    loads[4].wait()
     sv[...] = v_in[:, v_cols].astype(F32)
+    loads[5].wait()
     sg[...] = g_in[:, v_cols].astype(F32)
+    loads[6].wait()
     sq[...] = q_in[:, q_cols].astype(F32)
 
     pl.semaphore_wait(barrier, 22)
@@ -182,44 +200,67 @@
             y1_send.at[pair, kind], y1_recv.at[at_y, kind], seq_1=pair,
         )
 
-    def states(pair):
+    def place(pair, kind, i, slab):
+        rows = pl.ds(64 * i, 64)
+
+        @pl.when(pair == y)
+        def _():
+            yr[y, kind, rows] = slab
+
+        @pl.when(pair != y)
+        def _():
+            ys[pair, kind, rows] = slab
+
+    def hand_over(pair, kind):
+        @pl.when((pair != y) & sent(kind, y))
+        def _():
+            y1_copy(pair, kind, y).start()
+
+    def state_fwd(pair):
         vt[pair] = jnp.transpose(vb[:, pair_cols(pair)].astype(F32))
-        gt[pair] = jnp.transpose(gb[:, pair_cols(pair)].astype(F32))
         for i in range(2):
             head = pl.ds(pair * 2 + i, 1)
-            rows = pl.ds(64 * i, 64)
-            gate = fs[head, :]
-            value_hi, value_lo = split(vt[pair, rows] * de[head, :])
-            parts = [split(gt[pair, rows] * (gate * wts[level, head, :])) for level in (5, 3, 4)]
+            value_hi, value_lo = split(vt[pair, pl.ds(64 * i, 64)] * de[head, :])
             state = dot(
                 jnp.concatenate([value_hi, value_lo], axis=0), kb[:, head_cols(pair, i)], NN
             )
+            place(pair, 0, i, state[0:64] + state[64:128])
+            row = small[head, :]
+
+            @pl.when(pair == y)
+            def _():
+                yr[y, 0, 128 + i : 129 + i] = row
+
+            @pl.when(pair != y)
+            def _():
+                ys[pair, 0, 128 + i : 129 + i] = row
+
+        hand_over(pair, 0)
+
+    def state_back(pair):
+        gt[pair] = jnp.transpose(gb[:, pair_cols(pair)].astype(F32))
+        for i in range(2):
+            head = pl.ds(pair * 2 + i, 1)
+            hi, lo = split(gt[pair, pl.ds(64 * i, 64)] * (fs[head, :] * wts[5, head, :]))
+            back = dot(jnp.concatenate([hi, lo], axis=0), qb[:, head_cols(pair, i)], NN)
+            place(pair, 1, i, back[0:64] + back[64:128])
+        hand_over(pair, 1)
+
+    def state_near(pair):
+        for i in range(2):
+            head = pl.ds(pair * 2 + i, 1)
+            grad = gt[pair, pl.ds(64 * i, 64)]
+            parts = [split(grad * (fs[head, :] * wts[level, head, :])) for level in (3, 4)]
             back = dot(
                 jnp.concatenate([p[0] for p in parts] + [p[1] for p in parts], axis=0),
                 qb[:, head_cols(pair, i)], NN,
             )
-            slabs = [state[0:64] + state[64:128]] + [
-                back[64 * n : 64 * n + 64] + back[192 + 64 * n : 256 + 64 * n] for n in range(3)
-            ]
-            row = small[head, :]
-
-            @pl.when(pair == y)
-            def _():
-                for kind in range(4):
-                    yr[y, kind, rows] = slabs[kind]
-                yr[y, 0, 128 + i : 129 + i] = row
-
-            @pl.when(pair != y)
-            def _():
-                for kind in range(4):
-                    ys[pair, kind, rows] = slabs[kind]
-                ys[pair, 0, 128 + i : 129 + i] = row
-
-        for kind in range(4):
-
-            @pl.when((pair != y) & sent(kind, y))
-            def _():
-                y1_copy(pair, kind, y).start()
+            for n in range(2):
+                place(
+                    pair, 2 + n, i, back[64 * n : 64 * n + 64] + back[128 + 64 * n : 192 + 64 * n]
+                )
+        hand_over(pair, 2)
+        hand_over(pair, 3)
 
     def intra(pair):
         for i in range(2):
@@ -314,12 +355,14 @@
     def x_copy(to_x, kind):
         return remote(xs.at[kind], xr.at[x], x_send.at[to_x], x_recv.at[x], seq_0=to_x)
 
-    def combine_first():
+    def decays(i):
+        return [yr[n, 0, 128 + i : 129 + i] for n in range(4)]
+
+    def combine_fwd():
         y1_wait(0)
-        y1_wait(1)
         for i in range(2):
             rows = slice(64 * i, 64 * i + 64)
-            dec = [yr[n, 0, 128 + i : 129 + i] for n in range(4)]
+            dec = decays(i)
             both = dec[1] * yr[0, 0, rows] + yr[1, 0, rows]
             zs[2, 1, rows] = both
             after = dec[2] * both
@@ -328,18 +371,25 @@
             all_decay = dec[0] * dec[1] * (dec[2] * dec[3])
             xs[0, 128 + i : 129 + i] = all_decay
             xs[1, 128 + i : 129 + i] = all_decay
-
-            @pl.when(x > 0)
-            def _():
+        for to_x in range(4):
+
+            @pl.when(to_x > x)
+            def _():
+                x_copy(to_x, 0).start()
+
+    def combine_back():
+        y1_wait(1)
+
+        @pl.when(x > 0)
+        def _():
+            for i in range(2):
+                rows = slice(64 * i, 64 * i + 64)
+                dec = decays(i)
                 back = yr[2, 1, rows] + dec[2] * yr[3, 1, rows]
                 back = yr[1, 1, rows] + dec[1] * back
                 xs[1, rows] = yr[0, 1, rows] + dec[0] * back
 
         for to_x in range(4):
-
-            @pl.when(to_x > x)
-            def _():
-                x_copy(to_x, 0).start()
 
             @pl.when(to_x < x)
             def _():
@@ -350,29 +400,35 @@
         hand_back(2, 1)
         hand_back(3, 1)
 
-    def combine_second():
-        y1_wait(2)
-        y1_wait(3)
-
-        def take(at_x, acc):
-            remote(
-                xs.at[0], xr.at[at_x], x_send.at[at_x], x_recv.at[at_x], seq_0=at_x
-            ).wait_recv()
-            for i in range(2):
-                rows = slice(64 * i, 64 * i + 64)
-                acc[rows] = xr[at_x, 128 + i : 129 + i] * acc[rows] + xr[at_x, rows]
-
+    def take(acc, at_x):
+        remote(
+            xs.at[0], xr.at[at_x], x_send.at[at_x], x_recv.at[at_x], seq_0=at_x
+        ).wait_recv()
+        for i in range(2):
+            rows = slice(64 * i, 64 * i + 64)
+            acc[rows] = xr[at_x, 128 + i : 129 + i] * acc[rows] + xr[at_x, rows]
+
+    def enter_far():
         for at_x in range(4):
-            pl.when(at_x < x)(functools.partial(take, at_x, ein))
-        for at_x in range(3, -1, -1):
-            pl.when(at_x > x)(functools.partial(take, at_x, xin))
+            pl.when(at_x < x)(functools.partial(take, ein, at_x))
         for i in range(2):
             rows = slice(64 * i, 64 * i + 64)
-            dec = [yr[n, 0, 128 + i : 129 + i] for n in range(4)]
+            dec = decays(i)
             into = ein[rows]
             for at_y in range(4):
                 zs[at_y, 2, rows] = into
                 into = dec[at_y] * into
+        for at_y in range(4):
+            hand_back(at_y, 2)
+
+    def leave_far():
+        y1_wait(2)
+        y1_wait(3)
+        for at_x in range(3, -1, -1):
+            pl.when(at_x > x)(functools.partial(take, xin, at_x))
+        for i in range(2):
+            rows = slice(64 * i, 64 * i + 64)
+            dec = decays(i)
             late = xin[rows]
             zs[3, 3, rows] = late
             late = dec[3] * late
@@ -381,7 +437,6 @@
             zs[1, 3, rows] = late
             zs[0, 3, rows] = dec[1] * late + yr[1, 2, rows]
         for at_y in range(4):
-            hand_back(at_y, 2)
             hand_back(at_y, 3)
 
     def back_copy(pair, kind):
@@ -407,38 +462,49 @@
                 ).wait_recv()
 
         for i in range(2):
-            number = pair * 2 + i
-            head = pl.ds(number, 1)
+            head = pl.ds(pair * 2 + i, 1)
             rows = pl.ds(64 * i, 64)
-            query = qb[:, head_cols(pair, i)]
-            key = kb[:, head_cols(pair, i)]
             grad = gt[pair, rows]
             value = vt[pair, rows]
-            gate = fs[head, :]
-            end = de[head, :]
-            weight = [wts[level, head, :] for level in (3, 4, 5)]
-            enter = jnp.concatenate([zr[pair, n, rows] for n in range(3)], axis=0)
-            enter_hi, enter_lo = split(enter)
-            mixed = dot(jnp.concatenate([enter_hi, enter_lo], axis=0), query, NT)
+            enter_hi, enter_lo = split(
+                jnp.concatenate([zr[pair, n, rows] for n in range(3)], axis=0)
+            )
+            mixed = dot(
+                jnp.concatenate([enter_hi, enter_lo], axis=0), qb[:, head_cols(pair, i)], NT
+            )
             drift_row = drift[head, :]
             for n in range(3):
                 state_row = mixed[64 * n : 64 * n + 64] + mixed[192 + 64 * n : 256 + 64 * n]
-                level_row = gate * jnp.sum(state_row * grad, axis=0, keepdims=True)
+                level_row = fs[head, :] * jnp.sum(state_row * grad, axis=0, keepdims=True)
                 glw[3 + n, head, :] = level_row
-                drift_row = drift_row + weight[n] * level_row
+                drift_row = drift_row + wts[3 + n, head, :] * level_row
+            leave_hi, leave_lo = split(zr[pair, 3, rows])
+            left = dot(
+                jnp.concatenate([leave_hi, leave_lo], axis=0), kb[:, head_cols(pair, i)], NT
+            )
+            value_grad = gvt[pair, rows] + de[head, :] * (left[0:64] + left[64:128])
+            gvt[pair, rows] = value_grad
+            drift[head, :] = drift_row - jnp.sum(value * value_grad, axis=0, keepdims=True)
+
+    def cross_grad(pair):
+        for i in range(2):
+            head = pl.ds(pair * 2 + i, 1)
+            rows = pl.ds(64 * i, 64)
+            enter_hi, enter_lo = split(
+                jnp.concatenate([zr[pair, n, rows] for n in range(3)], axis=0)
+            )
+            grad = gt[pair, rows]
             weighted_hi, weighted_lo = split(
-                jnp.concatenate([grad * (gate * weight[n]) for n in range(3)], axis=0)
+                jnp.concatenate(
+                    [grad * (fs[head, :] * wts[3 + n, head, :]) for n in range(3)], axis=0
+                )
             )
             gq[:, head_cols(pair, i)] = gq[:, head_cols(pair, i)] + dot(
                 jnp.concatenate([weighted_hi, weighted_lo, weighted_hi], axis=0),
                 jnp.concatenate([enter_hi, enter_hi, enter_lo], axis=0), TN,
             )
             leave_hi, leave_lo = split(zr[pair, 3, rows])
-            left = dot(jnp.concatenate([leave_hi, leave_lo], axis=0), key, NT)
-            value_grad = gvt[pair, rows] + end * (left[0:64] + left[64:128])
-            gvt[pair, rows] = value_grad
-            drift[head, :] = drift_row - jnp.sum(value * value_grad, axis=0, keepdims=True)
-            ended_hi, ended_lo = split(value * end)
+            ended_hi, ended_lo = split(vt[pair, rows] * de[head, :])
             gk[:, head_cols(pair, i)] = gk[:, head_cols(pair, i)] + dot(
                 jnp.concatenate([ended_hi, ended_lo, ended_hi], axis=0),
                 jnp.concatenate([leave_hi, leave_hi, leave_lo], axis=0), TN,
@@ -460,13 +526,23 @@
 
         lax.fori_loop(low, high, step, 0)
 
-    loop(0, 4, states)
+    def toward(n):
+        return (y + jnp.where(n == 2, 3, jnp.where(n == 3, 0, 2 - n))) % 4
+
+    def nearby(n):
+        return (y + jnp.where(n == 2, 3, jnp.where(n == 3, 2, n))) % 4
+
+    loop(0, 4, lambda n: state_fwd(toward(n)))
+    loop(0, 4, lambda n: state_back(toward(n)))
+    loop(0, 4, lambda n: state_near(toward(n)))
     loop(0, 2, intra)
-    combine_first()
-    loop(2, 4, intra)
-    combine_second()
-    loop(0, 4, cross)
-
+    combine_fwd()
+    loop(2, 3, intra)
+    combine_back()
+    loop(3, 4, intra)
+    enter_far()
+    leave_far()
+    loop(0, 4, lambda n: cross(nearby(n)))
     lane = lax.broadcasted_iota(jnp.int32, (8, 256), 1)
     tail = suffix(drift[...], lane)
     drift[...] = tail
@@ -499,6 +575,7 @@
     for level in range(6):
         glw_out[level, own_heads, :] = glw[level, :, own_rows]
 
+    loop(0, 4, cross_grad)
     for pair in range(4):
         for kind in range(3):
             back_copy(pair, kind).wait_recv()
@@ -510,6 +587,15 @@
     glw_copy.wait_recv()
     for level in range(6):
         glw_out[level, other_heads, :] = bs[8 * level : 8 * level + 8, :]
+    stores = [
+        pltpu.make_async_copy(src, dst, store_sem.at[n])
+        for n, (src, dst) in enumerate((
+            (gq_out, gq_hbm), (gk_out, gk_hbm), (gv_out, gv_hbm), (glw_out, glw_hbm),
+            (glg_out, glg_hbm),
+        ))
+    ]
+    for store in stores[:4]:
+        store.start()
 
     for step in range(1, 16):
         peer = (chip + step) % 16
@@ -550,6 +636,7 @@
     bs_out.wait_recv()
     glg_out[other_heads, :] = (bs[48:56, :] + b_buf[z * 2 + other][:, 0:1]) * factor
 
+    stores[4].start()
     for swap in swaps:
         swap.wait_send()
     for pair in range(4):
@@ -581,14 +668,48 @@
         remote(
             b_buf.at[group], b_buf.at[group], b_send.at[peer], b_recv.at[group], **to
         ).wait_send()
+    for store in stores:
+        store.wait()
+
+
+def settle(*refs):
+    count = (len(refs) - 2) // 3
+    source, target, held = (refs[n * count : n * count + count] for n in range(3))
+    load_sem, store_sem = refs[3 * count :]
+    pieces = []
+    for n in range(count):
+        cuts = 4 if n < 2 else 2 if n == 2 else 1
+        rows = source[n].shape[0] // cuts
+        pieces += [(n, pl.ds(rows * cut, rows)) for cut in range(cuts)]
+    loads = [
+        pltpu.make_async_copy(source[n].at[at], held[n].at[at], load_sem.at[m])
+        for m, (n, at) in enumerate(pieces)
+    ]
+    stores = [
+        pltpu.make_async_copy(held[n].at[at], target[n].at[at], store_sem.at[m])
+        for m, (n, at) in enumerate(pieces)
+    ]
+    for load in loads:
+        load.start()
+    for load, store in zip(loads, stores):
+        load.wait()
+        store.start()
+    for store in stores:
+        store.wait()
 
 
 def shards(queries, keys, values, out_grad, log_gate, level_weight, doc_start):
-    vmem = pl.BlockSpec(memory_space=pltpu.VMEM)
-    scratch = (
-        [(128, 1024), (128, 1024), (128, 512), (128, 512), (64, 128)] * 2
+    args = (queries, keys, values, out_grad, log_gate, level_weight, doc_start.reshape(1, -1))
+    anywhere = pl.BlockSpec(memory_space=pl.ANY)
+    results = tuple(
+        jax.ShapeDtypeStruct(a.shape, a.dtype)
+        for a in (queries, keys, values, level_weight, log_gate)
     )
-    scratch = [pltpu.VMEM(s, F32) for s in scratch]
+    held = [pltpu.VMEM(r.shape, r.dtype) for r in results]
+    scratch = [pltpu.VMEM(a.shape, a.dtype) for a in args] + held
+    scratch += [pltpu.SemaphoreType.DMA((7,)), pltpu.SemaphoreType.DMA((5,))]
+    swap = [(128, 1024), (128, 1024), (128, 512), (128, 512), (64, 128)]
+    scratch += [pltpu.VMEM(s, F32) for s in swap * 2]
     scratch += [pltpu.VMEM(s, BF16) for s in ((256, 1024), (256, 1024), (256, 512), (256, 512))]
     scratch += [pltpu.VMEM((4, 128, 256), F32)] * 2
     scratch += [pltpu.VMEM((8, 256), F32)] * 5
@@ -606,22 +727,24 @@
     sems = [(5,), (5,), (4, 4), (4, 4), (4, 4), (4, 4), (4,), (4,), (4, 3), (4, 3), (2,), (2,)]
     sems += [(16,), (16,), (8,), (8,)]
     scratch += [pltpu.SemaphoreType.DMA(s) for s in sems]
-    return pl.pallas_call(
+    outs = pl.pallas_call(
         kernel,
-        out_shape=(
-            jax.ShapeDtypeStruct(queries.shape, BF16),
-            jax.ShapeDtypeStruct(keys.shape, BF16),
-            jax.ShapeDtypeStruct(values.shape, BF16),
-            jax.ShapeDtypeStruct(level_weight.shape, F32),
-            jax.ShapeDtypeStruct(log_gate.shape, F32),
-        ),
-        in_specs=[vmem] * 7,
-        out_specs=[vmem] * 5,
+        out_shape=results,
+        in_specs=[anywhere] * 7,
+        out_specs=[anywhere] * 5,
         scratch_shapes=scratch,
         compiler_params=pltpu.CompilerParams(
             collective_id=0, has_side_effects=True, vmem_limit_bytes=56 * 2**20
         ),
-    )(queries, keys, values, out_grad, log_gate, level_weight, doc_start.reshape(1, -1))
+    )(*args)
+    return pl.pallas_call(
+        settle,
+        out_shape=results,
+        in_specs=[anywhere] * 5,
+        out_specs=[anywhere] * 5,
+        scratch_shapes=held + [pltpu.SemaphoreType.DMA((12,)), pltpu.SemaphoreType.DMA((12,))],
+        compiler_params=pltpu.CompilerParams(vmem_limit_bytes=56 * 2**20),
+    )(*outs)
 
 
 def solution(mesh):

time: 58.6 us -> 49.9 us (0.85)
  local copies, waits for them, and re-layouts: 5.13 us -> 0 us
  Pallas kernels: 52.5 us -> 49.1 us
    unnamed x13 -> x0, local copies, waits for them, and re-layouts: 5.13 us -> none
    pallas_call x1 -> x2, Pallas kernels: 52.5 us -> 49.1 us  [the longest x1 46.9 us: shards(): pl.pallas_call(kernel, out_shape=results, in_specs=[anywhere] * 7, out_sp...]
where the time goes in v2:
time: 49.9 us; the launch traced here: 49.8 us
  Pallas kernels  49.1 us (98%)
  between operations  0.64 us (1%)
    pallas_call x1, Pallas kernels, shards(): pl.pallas_call(kernel, out_shape=results, in_specs=[anywhere] * 7, out_sp...  46.9 us
    pallas_call x1, Pallas kernels, shards(): pl.pallas_call(settle, out_shape=results, in_specs=[anywhere] * 5, out_sp...  2.25 us

profile of v2, /device:TPU:1, one launch (start us, length us, event | category | flops | bytes accessed | tf_op | source)
XLA Modules:
  0.0 49.8 jit_solution(6823100692917443977)
XLA Ops:
  0.6 46.9 %shard_map.110 = (bf16[128,2048]{1,0:T(8,128)(2,1)}, bf16[128,2048]{1,0:T(8,128)(2,1)}, bf16[128,1024]{1,0:T(8,128)(2,1)}, f32[6,16,128]{2,1,0:T(8,128)}, f32[16,128]{1,0:T(8,128)}) custom-call(bf16[128,2048]{1,0:T(8,128)(2,1)} %q_hbm.1, bf16[128,2048]{1,0:T(8,128)(2,1)} %k_hbm.1, bf16[128,1024]{1,0:T(8,128)(2,1)} %v_hbm.1, bf16[128,1024]{1,0:T(8,128)(2,1)} %g_hbm.1, ...), custom_call_target="tpu_custom_call" | custom-call | tf_op jit(solution)/shard_map/pallas_call | solution.py:730
  47.5 2.3 %shard_map.111 = (bf16[128,2048]{1,0:T(8,128)(2,1)}, bf16[128,2048]{1,0:T(8,128)(2,1)}, bf16[128,1024]{1,0:T(8,128)(2,1)}, f32[6,16,128]{2,1,0:T(8,128)}, f32[16,128]{1,0:T(8,128)}) custom-call(bf16[128,2048]{1,0:T(8,128)(2,1)} %get-tuple-element.10.refs_0_, bf16[128,2048]{1,0:T(8,128)(2,1)} %get-tuple-element.11.refs_1_, ...), custom_call_target="tpu_custom_call" | custom-call | tf_op jit(solution)/shard_map/pallas_call | solution.py:740

commit v3 on v2

--- a/solution.py
+++ b/solution.py
@@ -47,12 +47,11 @@
 
 def kernel(
     q_hbm, k_hbm, v_hbm, g_hbm, lg_hbm, lw_hbm, ds_hbm,
-    gq_hbm, gk_hbm, gv_hbm, glw_hbm, glg_hbm,
-    q_in, k_in, v_in, g_in, lg_in, lw_in, ds_in,
-    gq_out, gk_out, gv_out, glw_out, glg_out, load_sem, store_sem,
+    gq_out, gk_out, gv_out, glw_out, glg_out,
+    q_in, k_in, v_in, g_in, lg_in, lw_in, ds_in, load_sem,
     sq, sk, sv, sg, ss, rq, rk, rv, rg, rs,
     qb, kb, vb, gb, vt, gt,
-    gates, doc, cum, fs, de, wts, cm, bias, pt, rt,
+    gates, doc, cum, resets, fs, de, wts, cm, bias, pt, rt,
     gq, gk, gv, gvt, glw, drift, small,
     ys, yr, zs, zr, xs, xr, ein, xin,
     bq, bk, bv, bs,
@@ -157,32 +156,25 @@
     total = cum_now[:, 255:256]
     reset_total = reset[:, 255:256]
     cum[...] = cum_now
+    resets[...] = reset
     fs[...] = jnp.where(reset == 0.0, jnp.exp(cum_now), 0.0)
     de[...] = jnp.where(reset == reset_total, jnp.exp(total - cum_now), 0.0)
     decay = jnp.broadcast_to(jnp.where(reset_total == 0.0, jnp.exp(total), 0.0), (8, 128))
     small[...] = decay
-    columns = jnp.transpose(
-        jnp.concatenate([cum_now, reset, jnp.zeros((112, 256), F32)], axis=0)
-    )
-    for head in range(8):
-        cm[head] = jnp.broadcast_to(columns[:, head : head + 1], (256, 128))
-    reset_col = jnp.broadcast_to(columns[:, 8:9], (256, 128))
-    for half in range(2):
-        reset_row = jnp.broadcast_to(reset[0:1, 128 * half : 128 * half + 128], (256, 128))
-        s_pos = lax.broadcasted_iota(jnp.int32, (256, 128), 0)
-        t_pos = lax.broadcasted_iota(jnp.int32, (256, 128), 1) + 128 * half
-        bias[:, 128 * half : 128 * half + 128] = jnp.where(
-            (t_pos >= s_pos) & (reset_col == reset_row), 0.0, NEG
-        )
-
-    swaps[1].wait_recv()
-    kb[other_rows, :] = rk[...].astype(BF16)
-    swaps[2].wait_recv()
-    vb[other_rows, :] = rv[...].astype(BF16)
-    swaps[3].wait_recv()
-    gb[other_rows, :] = rg[...].astype(BF16)
-    swaps[4].wait_recv()
-    qb[other_rows, :] = rq[...].astype(BF16)
+    def masks():
+        columns = jnp.transpose(
+            jnp.concatenate([cum[...], resets[...], jnp.zeros((112, 256), F32)], axis=0)
+        )
+        for head in range(8):
+            cm[head] = jnp.broadcast_to(columns[:, head : head + 1], (256, 128))
+        reset_col = jnp.broadcast_to(columns[:, 8:9], (256, 128))
+        for half in range(2):
+            reset_row = jnp.broadcast_to(resets[0:1, 128 * half : 128 * half + 128], (256, 128))
+            s_pos = lax.broadcasted_iota(jnp.int32, (256, 128), 0)
+            t_pos = lax.broadcasted_iota(jnp.int32, (256, 128), 1) + 128 * half
+            bias[:, 128 * half : 128 * half + 128] = jnp.where(
+                (t_pos >= s_pos) & (reset_col == reset_row), 0.0, NEG
+            )
 
     def head_cols(pair, i):
         return pl.ds(pl.multiple_of(pair * 256 + i * 128, 128), 128)
@@ -418,8 +410,8 @@
             for at_y in range(4):
                 zs[at_y, 2, rows] = into
                 into = dec[at_y] * into
-        for at_y in range(4):
-            hand_back(at_y, 2)
+        for step in (2, 1, 3, 0):
+            hand_back((y + step) % 4, 2)
 
     def leave_far():
         y1_wait(2)
@@ -436,8 +428,8 @@
             late = dec[2] * late + (yr[2, 3, rows] + dec[2] * yr[3, 3, rows])
             zs[1, 3, rows] = late
             zs[0, 3, rows] = dec[1] * late + yr[1, 2, rows]
-        for at_y in range(4):
-            hand_back(at_y, 3)
+        for step in (2, 1, 3, 0):
+            hand_back((y + step) % 4, 3)
 
     def back_copy(pair, kind):
         if kind == 2:
@@ -447,11 +439,11 @@
             src, dst = ((gq, bq), (gk, bk))[kind]
         return remote(
             src.at[other_rows, cols], dst.at[:, cols],
-            out_send.at[pair, kind], out_recv.at[pair, kind], seq_2=other,
-        )
-
-    def cross(pair):
-        for kind in range(4):
+            out_send.at[kind], out_recv.at[kind], seq_2=other,
+        )
+
+    def y2_wait(pair, kinds):
+        for kind in kinds:
             here = (y % 2 == 1, y >= 2, x > 0, True)[kind]
 
             @pl.when((pair != y) & here)
@@ -461,11 +453,12 @@
                     y2_recv.at[pair, kind], seq_1=pair,
                 ).wait_recv()
 
+    def cross_in(pair):
+        y2_wait(pair, (0, 1, 2))
         for i in range(2):
             head = pl.ds(pair * 2 + i, 1)
             rows = pl.ds(64 * i, 64)
             grad = gt[pair, rows]
-            value = vt[pair, rows]
             enter_hi, enter_lo = split(
                 jnp.concatenate([zr[pair, n, rows] for n in range(3)], axis=0)
             )
@@ -478,22 +471,7 @@
                 level_row = fs[head, :] * jnp.sum(state_row * grad, axis=0, keepdims=True)
                 glw[3 + n, head, :] = level_row
                 drift_row = drift_row + wts[3 + n, head, :] * level_row
-            leave_hi, leave_lo = split(zr[pair, 3, rows])
-            left = dot(
-                jnp.concatenate([leave_hi, leave_lo], axis=0), kb[:, head_cols(pair, i)], NT
-            )
-            value_grad = gvt[pair, rows] + de[head, :] * (left[0:64] + left[64:128])
-            gvt[pair, rows] = value_grad
-            drift[head, :] = drift_row - jnp.sum(value * value_grad, axis=0, keepdims=True)
-
-    def cross_grad(pair):
-        for i in range(2):
-            head = pl.ds(pair * 2 + i, 1)
-            rows = pl.ds(64 * i, 64)
-            enter_hi, enter_lo = split(
-                jnp.concatenate([zr[pair, n, rows] for n in range(3)], axis=0)
-            )
-            grad = gt[pair, rows]
+            drift[head, :] = drift_row
             weighted_hi, weighted_lo = split(
                 jnp.concatenate(
                     [grad * (fs[head, :] * wts[3 + n, head, :]) for n in range(3)], axis=0
@@ -503,6 +481,30 @@
                 jnp.concatenate([weighted_hi, weighted_lo, weighted_hi], axis=0),
                 jnp.concatenate([enter_hi, enter_hi, enter_lo], axis=0), TN,
             )
+        back_copy(pair, 0).start()
+        wide = pl.ds(pl.multiple_of(pair * 256, 256), 256)
+        out_wide = pl.ds(pl.multiple_of(c * 1024 + pair * 256, 256), 256)
+        gq_out[:, out_wide] = gq[own_rows, wide].astype(BF16)
+
+    def cross_out(pair):
+        y2_wait(pair, (3,))
+        for i in range(2):
+            head = pl.ds(pair * 2 + i, 1)
+            rows = pl.ds(64 * i, 64)
+            leave_hi, leave_lo = split(zr[pair, 3, rows])
+            left = dot(
+                jnp.concatenate([leave_hi, leave_lo], axis=0), kb[:, head_cols(pair, i)], NT
+            )
+            value_grad = gvt[pair, rows] + de[head, :] * (left[0:64] + left[64:128])
+            gvt[pair, rows] = value_grad
+            drift[head, :] = drift[head, :] - jnp.sum(
+                vt[pair, rows] * value_grad, axis=0, keepdims=True
+            )
+
+    def cross_grad(pair):
+        for i in range(2):
+            head = pl.ds(pair * 2 + i, 1)
+            rows = pl.ds(64 * i, 64)
             leave_hi, leave_lo = split(zr[pair, 3, rows])
             ended_hi, ended_lo = split(vt[pair, rows] * de[head, :])
             gk[:, head_cols(pair, i)] = gk[:, head_cols(pair, i)] + dot(
@@ -510,12 +512,11 @@
                 jnp.concatenate([leave_hi, leave_hi, leave_lo], axis=0), TN,
             )
         gv[:, pair_cols(pair)] = jnp.transpose(gvt[pair])
-        for kind in range(3):
-            back_copy(pair, kind).start()
+        back_copy(pair, 1).start()
+        back_copy(pair, 2).start()
         wide = pl.ds(pl.multiple_of(pair * 256, 256), 256)
         out_wide = pl.ds(pl.multiple_of(c * 1024 + pair * 256, 256), 256)
         out_narrow = pl.ds(pl.multiple_of(c * 512 + pair * 128, 128), 128)
-        gq_out[:, out_wide] = gq[own_rows, wide].astype(BF16)
         gk_out[:, out_wide] = gk[own_rows, wide].astype(BF16)
         gv_out[:, out_narrow] = gv[own_rows, pair_cols(pair)].astype(BF16)
 
@@ -532,17 +533,27 @@
     def nearby(n):
         return (y + jnp.where(n == 2, 3, jnp.where(n == 3, 2, n))) % 4
 
+    swaps[1].wait_recv()
+    kb[other_rows, :] = rk[...].astype(BF16)
+    swaps[2].wait_recv()
+    vb[other_rows, :] = rv[...].astype(BF16)
     loop(0, 4, lambda n: state_fwd(toward(n)))
+    swaps[3].wait_recv()
+    gb[other_rows, :] = rg[...].astype(BF16)
+    swaps[4].wait_recv()
+    qb[other_rows, :] = rq[...].astype(BF16)
     loop(0, 4, lambda n: state_back(toward(n)))
+    masks()
+    loop(0, 1, intra)
+    combine_fwd()
     loop(0, 4, lambda n: state_near(toward(n)))
-    loop(0, 2, intra)
-    combine_fwd()
-    loop(2, 3, intra)
     combine_back()
+    loop(1, 3, intra)
+    enter_far()
     loop(3, 4, intra)
-    enter_far()
     leave_far()
-    loop(0, 4, lambda n: cross(nearby(n)))
+    loop(0, 4, lambda n: cross_in(nearby(n)))
+    loop(0, 4, lambda n: cross_out(nearby(n)))
     lane = lax.broadcasted_iota(jnp.int32, (8, 256), 1)
     tail = suffix(drift[...], lane)
     drift[...] = tail
@@ -556,7 +567,7 @@
     def a_copy(step):
         peer = (chip + step) % 16
         return remote(
-            a_buf.at[chip], a_buf.at[chip], a_send.at[peer], a_recv.at[chip],
+            a_buf.at[chip], a_buf.at[chip], a_send.at[0], a_recv.at[0],
             seq_0=peer // 4, seq_1=peer % 4,
         )
 
@@ -576,9 +587,14 @@
         glw_out[level, own_heads, :] = glw[level, :, own_rows]
 
     loop(0, 4, cross_grad)
-    for pair in range(4):
-        for kind in range(3):
-            back_copy(pair, kind).wait_recv()
+    def back_whole(kind):
+        src, dst = ((gq, bq), (gk, bk), (gv, bv))[kind]
+        return remote(
+            src.at[other_rows, :], dst, out_send.at[kind], out_recv.at[kind], seq_2=other
+        )
+
+    for kind in range(3):
+        back_whole(kind).wait_recv()
     other_q = pl.ds(pl.multiple_of(other * 1024, 1024), 1024)
     other_v = pl.ds(pl.multiple_of(other * 512, 512), 512)
     gq_out[:, other_q] = bq[...].astype(BF16)
@@ -587,22 +603,11 @@
     glw_copy.wait_recv()
     for level in range(6):
         glw_out[level, other_heads, :] = bs[8 * level : 8 * level + 8, :]
-    stores = [
-        pltpu.make_async_copy(src, dst, store_sem.at[n])
-        for n, (src, dst) in enumerate((
-            (gq_out, gq_hbm), (gk_out, gk_hbm), (gv_out, gv_hbm), (glw_out, glw_hbm),
-            (glg_out, glg_hbm),
-        ))
-    ]
-    for store in stores[:4]:
-        store.start()
-
-    for step in range(1, 16):
-        peer = (chip + step) % 16
-        remote(
-            a_buf.at[chip], a_buf.at[peer], a_send.at[peer], a_recv.at[peer],
-            seq_0=peer // 4, seq_1=peer % 4,
-        ).wait_recv()
+
+    a_whole = remote(
+        a_buf.at[pl.ds(0, 15)], a_buf.at[pl.ds(0, 15)], a_send.at[0], a_recv.at[0], seq_2=other
+    )
+    a_whole.wait_recv()
     run = jnp.zeros((8, 1), F32)
     later = jnp.zeros((8, 1), F32)
     squares = jnp.zeros((8, 1), F32)
@@ -616,18 +621,17 @@
 
     def b_peer(step):
         peer = (group + step) % 8
-        return peer, {"head": peer // 2, "seq_2": peer % 2}
+        return {"head": peer // 2, "seq_2": peer % 2}
 
     for step in range(1, 8):
-        peer, to = b_peer(step)
+        to = b_peer(step)
         remote(
-            b_buf.at[group], b_buf.at[group], b_send.at[peer], b_recv.at[group], **to
+            b_buf.at[group], b_buf.at[group], b_send.at[0], b_recv.at[0], **to
         ).start()
-    for step in range(1, 8):
-        peer, to = b_peer(step)
-        remote(
-            b_buf.at[group], b_buf.at[peer], b_send.at[peer], b_recv.at[peer], **to
-        ).wait_recv()
+    b_whole = remote(
+        b_buf.at[pl.ds(0, 7)], b_buf.at[pl.ds(0, 7)], b_send.at[0], b_recv.at[0], seq_2=other
+    )
+    b_whole.wait_recv()
     total_square = jnp.zeros((8, 128), F32)
     for at in range(8):
         total_square = total_square + b_buf[at]
@@ -636,7 +640,6 @@
     bs_out.wait_recv()
     glg_out[other_heads, :] = (bs[48:56, :] + b_buf[z * 2 + other][:, 0:1]) * factor
 
-    stores[4].start()
     for swap in swaps:
         swap.wait_send()
     for pair in range(4):
@@ -657,42 +660,26 @@
         def _():
             x_copy(pair, 0).wait_send()
 
-        for kind in range(3):
-            back_copy(pair, kind).wait_send()
+    for kind in range(3):
+        back_whole(kind).wait_send()
     glw_copy.wait_send()
     bs_out.wait_send()
-    for step in range(1, 16):
-        a_copy(step).wait_send()
-    for step in range(1, 8):
-        peer, to = b_peer(step)
-        remote(
-            b_buf.at[group], b_buf.at[group], b_send.at[peer], b_recv.at[group], **to
-        ).wait_send()
-    for store in stores:
-        store.wait()
+    a_whole.wait_send()
+    b_whole.wait_send()
 
 
 def settle(*refs):
-    count = (len(refs) - 2) // 3
-    source, target, held = (refs[n * count : n * count + count] for n in range(3))
-    load_sem, store_sem = refs[3 * count :]
-    pieces = []
-    for n in range(count):
+    source, target, sem = refs[:5], refs[5:10], refs[10]
+    stores = []
+    for n in range(5):
         cuts = 4 if n < 2 else 2 if n == 2 else 1
         rows = source[n].shape[0] // cuts
-        pieces += [(n, pl.ds(rows * cut, rows)) for cut in range(cuts)]
-    loads = [
-        pltpu.make_async_copy(source[n].at[at], held[n].at[at], load_sem.at[m])
-        for m, (n, at) in enumerate(pieces)
-    ]
-    stores = [
-        pltpu.make_async_copy(held[n].at[at], target[n].at[at], store_sem.at[m])
-        for m, (n, at) in enumerate(pieces)
-    ]
-    for load in loads:
-        load.start()
-    for load, store in zip(loads, stores):
-        load.wait()
+        for m in range(cuts):
+            at = pl.ds(rows * m, rows)
+            stores.append(
+                pltpu.make_async_copy(source[n].at[at], target[n].at[at], sem.at[len(stores)])
+            )
+    for store in stores:
         store.start()
     for store in stores:
         store.wait()
@@ -705,14 +692,13 @@
         jax.ShapeDtypeStruct(a.shape, a.dtype)
         for a in (queries, keys, values, level_weight, log_gate)
     )
-    held = [pltpu.VMEM(r.shape, r.dtype) for r in results]
-    scratch = [pltpu.VMEM(a.shape, a.dtype) for a in args] + held
-    scratch += [pltpu.SemaphoreType.DMA((7,)), pltpu.SemaphoreType.DMA((5,))]
+    held = tuple(pltpu.VMEM(r.shape, r.dtype) for r in results)
+    scratch = [pltpu.VMEM(a.shape, a.dtype) for a in args] + [pltpu.SemaphoreType.DMA((7,))]
     swap = [(128, 1024), (128, 1024), (128, 512), (128, 512), (64, 128)]
     scratch += [pltpu.VMEM(s, F32) for s in swap * 2]
     scratch += [pltpu.VMEM(s, BF16) for s in ((256, 1024), (256, 1024), (256, 512), (256, 512))]
     scratch += [pltpu.VMEM((4, 128, 256), F32)] * 2
-    scratch += [pltpu.VMEM((8, 256), F32)] * 5
+    scratch += [pltpu.VMEM((8, 256), F32)] * 6
     scratch += [pltpu.VMEM((6, 8, 256), F32), pltpu.VMEM((8, 256, 128), F32)]
     scratch += [pltpu.VMEM((256, 256), F32), pltpu.VMEM((256, 256), BF16), pltpu.VMEM((256, 256), BF16)]
     scratch += [pltpu.VMEM((256, 1024), F32), pltpu.VMEM((256, 1024), F32), pltpu.VMEM((256, 512), F32)]
@@ -724,17 +710,17 @@
     scratch += [pltpu.VMEM((128, 1024), F32), pltpu.VMEM((128, 1024), F32), pltpu.VMEM((128, 512), F32)]
     scratch += [pltpu.VMEM((56, 128), F32)]
     scratch += [pltpu.VMEM((16, 8, 128), F32), pltpu.VMEM((8, 8, 128), F32)]
-    sems = [(5,), (5,), (4, 4), (4, 4), (4, 4), (4, 4), (4,), (4,), (4, 3), (4, 3), (2,), (2,)]
-    sems += [(16,), (16,), (8,), (8,)]
+    sems = [(5,), (5,), (4, 4), (4, 4), (4, 4), (4, 4), (4,), (4,), (3,), (3,), (2,), (2,)]
+    sems += [(1,)] * 4
     scratch += [pltpu.SemaphoreType.DMA(s) for s in sems]
     outs = pl.pallas_call(
         kernel,
-        out_shape=results,
+        out_shape=held,
         in_specs=[anywhere] * 7,
-        out_specs=[anywhere] * 5,
+        out_specs=[pl.BlockSpec(memory_space=pltpu.VMEM)] * 5,
         scratch_shapes=scratch,
         compiler_params=pltpu.CompilerParams(
-            collective_id=0, has_side_effects=True, vmem_limit_bytes=56 * 2**20
+            collective_id=0, has_side_effects=True, vmem_limit_bytes=60 * 2**20
         ),
     )(*args)
     return pl.pallas_call(
@@ -742,8 +728,8 @@
         out_shape=results,
         in_specs=[anywhere] * 5,
         out_specs=[anywhere] * 5,
-        scratch_shapes=held + [pltpu.SemaphoreType.DMA((12,)), pltpu.SemaphoreType.DMA((12,))],
-        compiler_params=pltpu.CompilerParams(vmem_limit_bytes=56 * 2**20),
+        scratch_shapes=[pltpu.SemaphoreType.DMA((12,))],
+        compiler_params=pltpu.CompilerParams(vmem_limit_bytes=48 * 2**20),
     )(*outs)
 
 

time: 49.9 us -> 46.8 us (0.938)
  Pallas kernels: 49.1 us -> 46 us
    pallas_call x1, Pallas kernels: 46.9 us -> 44.8 us  [shards(): pl.pallas_call(kernel, out_shape=held, in_specs=[anywhere] * 7, out_specs...]
    pallas_call x1, Pallas kernels: 2.25 us -> 1.16 us  [shards(): pl.pallas_call(settle, out_shape=results, in_specs=[anywhere] * 5, out_sp...]
where the time goes in v3:
time: 46.8 us; the launch traced here: 46.6 us
  Pallas kernels  46 us (98%)
  between operations  0.64 us (1%)
    pallas_call x1, Pallas kernels, shards(): pl.pallas_call(kernel, out_shape=held, in_specs=[anywhere] * 7, out_specs...  44.8 us
    pallas_call x1, Pallas kernels, shards(): pl.pallas_call(settle, out_shape=results, in_specs=[anywhere] * 5, out_sp...  1.16 us

profile of v3, /device:TPU:1, one launch (start us, length us, event | category | flops | bytes accessed | tf_op | source)
XLA Modules:
  0.0 46.6 jit_solution(12961379191977292608)
XLA Ops:
  0.6 44.8 %shard_map.110 = (bf16[128,2048]{1,0:T(8,128)(2,1)S(1)}, bf16[128,2048]{1,0:T(8,128)(2,1)S(1)}, bf16[128,1024]{1,0:T(8,128)(2,1)S(1)}, f32[6,16,128]{2,1,0:T(8,128)S(1)}, f32[16,128]{1,0:T(8,128)S(1)}) custom-call(bf16[128,2048]{1,0:T(8,128)(2,1)} %q_hbm.1, bf16[128,2048]{1,0:T(8,128)(2,1)} %k_hbm.1, bf16[128,1024]{1,0:T(8,128)(2,1)} %v_hbm.1, ...), custom_call_target="tpu_custom_call" | custom-call | tf_op jit(solution)/shard_map/pallas_call | solution.py:716
  45.5 1.2 %shard_map.111 = (bf16[128,2048]{1,0:T(8,128)(2,1)}, bf16[128,2048]{1,0:T(8,128)(2,1)}, bf16[128,1024]{1,0:T(8,128)(2,1)}, f32[6,16,128]{2,1,0:T(8,128)}, f32[16,128]{1,0:T(8,128)}) custom-call(bf16[128,2048]{1,0:T(8,128)(2,1)S(1)} %get-tuple-element.10.refs_0_, bf16[128,2048]{1,0:T(8,128)(2,1)S(1)} %get-tuple-element.11.refs_1_, ...), custom_call_target="tpu_custom_call" | custom-call | tf_op jit(solution)/shard_map/pallas_call | solution.py:726

commit v4 on v3

--- a/solution.py
+++ b/solution.py
@@ -81,11 +81,11 @@
         load.start()
 
     barrier = pltpu.get_barrier_semaphore()
-    for step in range(1, 16):
-        peer = (chip + step) % 16
-        pl.semaphore_signal(
-            barrier, inc=1, device_id={"seq_0": peer // 4, "seq_1": peer % 4}, device_id_type=MESH
-        )
+    for step in range(1, 4):
+        for axis, place in (("seq_1", y), ("seq_0", x)):
+            pl.semaphore_signal(
+                barrier, inc=1, device_id={axis: (place + step) % 4}, device_id_type=MESH
+            )
     for step in range(1, 8):
         peer = (group + step) % 8
         pl.semaphore_signal(
@@ -116,7 +116,7 @@
     loads[6].wait()
     sq[...] = q_in[:, q_cols].astype(F32)
 
-    pl.semaphore_wait(barrier, 22)
+    pl.semaphore_wait(barrier, 13)
     swaps = [
         remote(src, dst, in_send.at[n], in_recv.at[n], seq_2=other)
         for n, (src, dst) in enumerate(((ss, rs), (sk, rk), (sv, rv), (sg, rg), (sq, rq)))
@@ -369,6 +369,11 @@
             def _():
                 x_copy(to_x, 0).start()
 
+        hand_back(1, 0)
+        hand_back(3, 0)
+        hand_back(2, 1)
+        hand_back(3, 1)
+
     def combine_back():
         y1_wait(1)
 
@@ -387,10 +392,6 @@
             def _():
                 x_copy(to_x, 1).start()
 
-        hand_back(1, 0)
-        hand_back(3, 0)
-        hand_back(2, 1)
-        hand_back(3, 1)
 
     def take(acc, at_x):
         remote(
@@ -543,10 +544,10 @@
     swaps[4].wait_recv()
     qb[other_rows, :] = rq[...].astype(BF16)
     loop(0, 4, lambda n: state_back(toward(n)))
+    loop(0, 4, lambda n: state_near(toward(n)))
+    combine_fwd()
     masks()
     loop(0, 1, intra)
-    combine_fwd()
-    loop(0, 4, lambda n: state_near(toward(n)))
     combine_back()
     loop(1, 3, intra)
     enter_far()

time: 46.8 us -> 45.4 us (0.970)
  Pallas kernels: 46 us -> 44.6 us
    pallas_call x1, Pallas kernels: 44.8 us -> 43.5 us  [shards(): pl.pallas_call(kernel, out_shape=held, in_specs=[anywhere] * 7, out_specs...]
where the time goes in v4:
time: 45.4 us; the launch traced here: 45.3 us
  Pallas kernels  44.6 us (98%)
  between operations  0.64 us (1%)
    pallas_call x1, Pallas kernels, shards(): pl.pallas_call(kernel, out_shape=held, in_specs=[anywhere] * 7, out_specs...  43.5 us
    pallas_call x1, Pallas kernels, shards(): pl.pallas_call(settle, out_shape=results, in_specs=[anywhere] * 5, out_sp...  1.16 us

profile of v4, /device:TPU:1, one launch (start us, length us, event | category | flops | bytes accessed | tf_op | source)
XLA Modules:
  0.0 45.3 jit_solution(1757784999472617966)
XLA Ops:
  0.6 43.5 %shard_map.110 = (bf16[128,2048]{1,0:T(8,128)(2,1)S(1)}, bf16[128,2048]{1,0:T(8,128)(2,1)S(1)}, bf16[128,1024]{1,0:T(8,128)(2,1)S(1)}, f32[6,16,128]{2,1,0:T(8,128)S(1)}, f32[16,128]{1,0:T(8,128)S(1)}) custom-call(bf16[128,2048]{1,0:T(8,128)(2,1)} %q_hbm.1, bf16[128,2048]{1,0:T(8,128)(2,1)} %k_hbm.1, bf16[128,1024]{1,0:T(8,128)(2,1)} %v_hbm.1, ...), custom_call_target="tpu_custom_call" | custom-call | tf_op jit(solution)/shard_map/pallas_call | solution.py:717
  44.1 1.2 %shard_map.111 = (bf16[128,2048]{1,0:T(8,128)(2,1)}, bf16[128,2048]{1,0:T(8,128)(2,1)}, bf16[128,1024]{1,0:T(8,128)(2,1)}, f32[6,16,128]{2,1,0:T(8,128)}, f32[16,128]{1,0:T(8,128)}) custom-call(bf16[128,2048]{1,0:T(8,128)(2,1)S(1)} %get-tuple-element.10.refs_0_, bf16[128,2048]{1,0:T(8,128)(2,1)S(1)} %get-tuple-element.11.refs_1_, ...), custom_call_target="tpu_custom_call" | custom-call | tf_op jit(solution)/shard_map/pallas_call | solution.py:727

commit v5 on v4

--- a/solution.py
+++ b/solution.py
@@ -55,9 +55,9 @@
     gq, gk, gv, gvt, glw, drift, small,
     ys, yr, zs, zr, xs, xr, ein, xin,
     bq, bk, bv, bs,
-    a_buf, b_buf,
+    a_buf,
     in_send, in_recv, y1_send, y1_recv, y2_send, y2_recv, x_send, x_recv,
-    out_send, out_recv, last_send, last_recv, a_send, a_recv, b_send, b_recv,
+    out_send, out_recv, last_send, last_recv, a_send, a_recv,
 ):
     x, y, c, z = (lax.axis_index(n) for n in ("seq_0", "seq_1", "seq_2", "head"))
     other = 1 - c
@@ -100,6 +100,10 @@
     other_rows = pl.ds(pl.multiple_of(other * 128, 128), 128)
     own_heads = pl.ds(pl.multiple_of(c * 8, 8), 8)
     other_heads = pl.ds(pl.multiple_of(other * 8, 8), 8)
+    swaps = [
+        remote(src, dst, in_send.at[n], in_recv.at[n], seq_2=other)
+        for n, (src, dst) in enumerate(((ss, rs), (sk, rk), (sv, rv), (sg, rg), (sq, rq)))
+    ]
     for load in loads[:3]:
         load.wait()
     ds_row = jnp.broadcast_to(ds_in[...].astype(F32), (8, 128))
@@ -111,19 +115,15 @@
     sk[...] = k_in[:, q_cols].astype(F32)
     loads[4].wait()
     sv[...] = v_in[:, v_cols].astype(F32)
+    pl.semaphore_wait(barrier, 13)
+    for swap in swaps[:3]:
+        swap.start()
     loads[5].wait()
     sg[...] = g_in[:, v_cols].astype(F32)
     loads[6].wait()
     sq[...] = q_in[:, q_cols].astype(F32)
-
-    pl.semaphore_wait(barrier, 13)
-    swaps = [
-        remote(src, dst, in_send.at[n], in_recv.at[n], seq_2=other)
-        for n, (src, dst) in enumerate(((ss, rs), (sk, rk), (sv, rv), (sg, rg), (sq, rq)))
-    ]
-    for swap in swaps:
+    for swap in swaps[3:]:
         swap.start()
-
     kb[own_rows, :] = k_in[:, own_q]
     vb[own_rows, :] = v_in[:, own_v]
     gb[own_rows, :] = g_in[:, own_v]
@@ -560,20 +560,30 @@
     drift[...] = tail
     bs_out = remote(small.at[:, :], bs.at[pl.ds(48, 8), :], last_send.at[1], last_recv.at[1], seq_2=other)
     tile = lax.broadcasted_iota(jnp.int32, (8, 128), 1)
-    head_total = jnp.broadcast_to(tail[:, 0:1], (8, 128))
-    head_square = jnp.broadcast_to(jnp.sum(tail * tail, axis=1, keepdims=True), (8, 128))
-    head_sum = jnp.broadcast_to(jnp.sum(tail, axis=1, keepdims=True), (8, 128))
-    a_buf[chip] = jnp.where(tile == 0, head_total, jnp.where(tile == 1, head_square, head_sum))
-
-    def a_copy(step):
-        peer = (chip + step) % 16
+    mine = lax.broadcasted_iota(jnp.int32, (8, 128), 0)
+    head_total = tail[:, 0:1]
+    head_square = jnp.sum(tail * tail, axis=1, keepdims=True)
+    head_sum = jnp.sum(tail, axis=1, keepdims=True)
+    slots = [
+        jnp.where(tile == mine + 8 * n, jnp.broadcast_to(part, (8, 128)), 0.0)
+        for n, part in enumerate((head_total, head_square, head_sum))
+    ]
+    place_here = chip * 8 + group
+    a_buf[place_here] = jnp.sum(slots[0] + slots[1] + slots[2], axis=0, keepdims=True)
+
+    def a_copy(dx, dy, dz, dc):
         return remote(
-            a_buf.at[chip], a_buf.at[chip], a_send.at[0], a_recv.at[0],
-            seq_0=peer // 4, seq_1=peer % 4,
-        )
-
-    for step in range(1, 16):
-        a_copy(step).start()
+            a_buf.at[place_here], a_buf.at[place_here], a_send.at[0], a_recv.at[0],
+            seq_0=(x + dx) % 4, seq_1=(y + dy) % 4, seq_2=(c + dc) % 2, head=(z + dz) % 4,
+        )
+
+    def hops(move):
+        return -(sum(min(d, 4 - d) for d in move[:3]) + 0.5 * move[3])
+
+    moves = [(dx, dy, dz, dc) for dx in range(4) for dy in range(4) for dz in range(4) for dc in (0, 1)]
+    for move in sorted(moves, key=hops):
+        if any(move):
+            a_copy(*move).start()
     small[...] = drift[:, other_rows]
     for level in range(6):
         ss_rows = slice(8 * level, 8 * level + 8)
@@ -606,40 +616,32 @@
         glw_out[level, other_heads, :] = bs[8 * level : 8 * level + 8, :]
 
     a_whole = remote(
-        a_buf.at[pl.ds(0, 15)], a_buf.at[pl.ds(0, 15)], a_send.at[0], a_recv.at[0], seq_2=other
+        a_buf.at[pl.ds(0, 127)], a_buf.at[pl.ds(0, 127)], a_send.at[0], a_recv.at[0], seq_2=other
     )
     a_whole.wait_recv()
-    run = jnp.zeros((8, 1), F32)
-    later = jnp.zeros((8, 1), F32)
-    squares = jnp.zeros((8, 1), F32)
+    run = jnp.zeros((8, 128), F32)
+    later = jnp.zeros((8, 128), F32)
+    squares = jnp.zeros((8, 128), F32)
     for at in range(15, -1, -1):
-        now = a_buf[at]
+        now = a_buf[8 * at : 8 * at + 8, 0, :]
         later = later + run * (chip == at).astype(F32)
-        squares = squares + now[:, 1:2] + run * (2.0 * now[:, 2:3] + 256.0 * run)
-        run = run + now[:, 0:1]
-    whole = jnp.broadcast_to(jnp.sum(squares, axis=0, keepdims=True), (8, 128))
-    b_buf[group] = jnp.where(tile < 64, jnp.broadcast_to(later, (8, 128)), whole)
-
-    def b_peer(step):
-        peer = (group + step) % 8
-        return {"head": peer // 2, "seq_2": peer % 2}
-
-    for step in range(1, 8):
-        to = b_peer(step)
-        remote(
-            b_buf.at[group], b_buf.at[group], b_send.at[0], b_recv.at[0], **to
-        ).start()
-    b_whole = remote(
-        b_buf.at[pl.ds(0, 7)], b_buf.at[pl.ds(0, 7)], b_send.at[0], b_recv.at[0], seq_2=other
-    )
-    b_whole.wait_recv()
-    total_square = jnp.zeros((8, 128), F32)
-    for at in range(8):
-        total_square = total_square + b_buf[at]
-    factor = jnp.minimum(1.0, lax.rsqrt(total_square[:, 64:65] / (64 * 4096) + 1e-06))
-    glg_out[own_heads, :] = (drift[:, own_rows] + later) * factor
+        square = pltpu.roll(now, 120, 1)
+        total_of = pltpu.roll(now, 112, 1)
+        squares = squares + square + run * (2.0 * total_of + 256.0 * run)
+        run = run + now
+    squares = jnp.where(tile < 8, squares, 0.0)
+    total_square = jnp.sum(jnp.sum(squares, axis=1, keepdims=True), axis=0, keepdims=True)
+    factor = jnp.minimum(1.0, lax.rsqrt(total_square / (64 * 4096) + 1e-06))
+
+    def later_of(at_group):
+        row = jnp.sum(jnp.where(mine == at_group, later, 0.0), axis=0, keepdims=True)
+        return jnp.sum(
+            jnp.where(tile == mine, jnp.broadcast_to(row, (8, 128)), 0.0), axis=1, keepdims=True
+        )
+
+    glg_out[own_heads, :] = (drift[:, own_rows] + later_of(group)) * factor
     bs_out.wait_recv()
-    glg_out[other_heads, :] = (bs[48:56, :] + b_buf[z * 2 + other][:, 0:1]) * factor
+    glg_out[other_heads, :] = (bs[48:56, :] + later_of(z * 2 + other)) * factor
 
     for swap in swaps:
         swap.wait_send()
@@ -666,7 +668,6 @@
     glw_copy.wait_send()
     bs_out.wait_send()
     a_whole.wait_send()
-    b_whole.wait_send()
 
 
 def settle(*refs):
@@ -710,9 +711,9 @@
     scratch += [pltpu.VMEM((128, 128), F32)] * 2
     scratch += [pltpu.VMEM((128, 1024), F32), pltpu.VMEM((128, 1024), F32), pltpu.VMEM((128, 512), F32)]
     scratch += [pltpu.VMEM((56, 128), F32)]
-    scratch += [pltpu.VMEM((16, 8, 128), F32), pltpu.VMEM((8, 8, 128), F32)]
+    scratch += [pltpu.VMEM((128, 1, 128), F32)]
     sems = [(5,), (5,), (4, 4), (4, 4), (4, 4), (4, 4), (4,), (4,), (3,), (3,), (2,), (2,)]
-    sems += [(1,)] * 4
+    sems += [(1,)] * 2
     scratch += [pltpu.SemaphoreType.DMA(s) for s in sems]
     outs = pl.pallas_call(
         kernel,

time: 45.4 us -> 42.5 us (0.936)
  Pallas kernels: 44.6 us -> 41.8 us
    pallas_call x1, Pallas kernels: 43.5 us -> 40.6 us  [shards(): pl.pallas_call(kernel, out_shape=held, in_specs=[anywhere] * 7, out_specs...]
where the time goes in v5:
time: 42.5 us; the launch traced here: 42.4 us
  Pallas kernels  41.8 us (98%)
  between operations  0.64 us (2%)
    pallas_call x1, Pallas kernels, shards(): pl.pallas_call(kernel, out_shape=held, in_specs=[anywhere] * 7, out_specs...  40.6 us
    pallas_call x1, Pallas kernels, shards(): pl.pallas_call(settle, out_shape=results, in_specs=[anywhere] * 5, out_sp...  1.16 us

profile of v5, /device:TPU:1, one launch (start us, length us, event | category | flops | bytes accessed | tf_op | source)
XLA Modules:
  0.0 42.4 jit_solution(5243770259199867700)
XLA Ops:
  0.6 40.6 %shard_map.110 = (bf16[128,2048]{1,0:T(8,128)(2,1)S(1)}, bf16[128,2048]{1,0:T(8,128)(2,1)S(1)}, bf16[128,1024]{1,0:T(8,128)(2,1)S(1)}, f32[6,16,128]{2,1,0:T(8,128)S(1)}, f32[16,128]{1,0:T(8,128)S(1)}) custom-call(bf16[128,2048]{1,0:T(8,128)(2,1)} %q_hbm.1, bf16[128,2048]{1,0:T(8,128)(2,1)} %k_hbm.1, bf16[128,1024]{1,0:T(8,128)(2,1)} %v_hbm.1, ...), custom_call_target="tpu_custom_call" | custom-call | tf_op jit(solution)/shard_map/pallas_call | solution.py:718
  41.2 1.2 %shard_map.111 = (bf16[128,2048]{1,0:T(8,128)(2,1)}, bf16[128,2048]{1,0:T(8,128)(2,1)}, bf16[128,1024]{1,0:T(8,128)(2,1)}, f32[6,16,128]{2,1,0:T(8,128)}, f32[16,128]{1,0:T(8,128)}) custom-call(bf16[128,2048]{1,0:T(8,128)(2,1)S(1)} %get-tuple-element.10.refs_0_, bf16[128,2048]{1,0:T(8,128)(2,1)S(1)} %get-tuple-element.11.refs_1_, ...), custom_call_target="tpu_custom_call" | custom-call | tf_op jit(solution)/shard_map/pallas_call | solution.py:728

commit v6 on v5

--- a/solution.py
+++ b/solution.py
@@ -56,7 +56,7 @@
     ys, yr, zs, zr, xs, xr, ein, xin,
     bq, bk, bv, bs,
     a_buf,
-    in_send, in_recv, y1_send, y1_recv, y2_send, y2_recv, x_send, x_recv,
+    in_send, in_recv, kv_send, kv_recv, y1_send, y1_recv, y2_send, y2_recv, x_send, x_recv,
     out_send, out_recv, last_send, last_recv, a_send, a_recv,
 ):
     x, y, c, z = (lax.axis_index(n) for n in ("seq_0", "seq_1", "seq_2", "head"))
@@ -102,8 +102,27 @@
     other_heads = pl.ds(pl.multiple_of(other * 8, 8), 8)
     swaps = [
         remote(src, dst, in_send.at[n], in_recv.at[n], seq_2=other)
-        for n, (src, dst) in enumerate(((ss, rs), (sk, rk), (sv, rv), (sg, rg), (sq, rq)))
+        for n, (src, dst) in enumerate(((ss, rs), (sg, rg), (sq, rq)))
     ]
+
+    def toward(n):
+        return (y + jnp.where(n == 2, 3, jnp.where(n == 3, 0, 2 - n))) % 4
+
+    def nearby(n):
+        return (y + jnp.where(n == 2, 3, jnp.where(n == 3, 2, n))) % 4
+
+    def key_copy(pair):
+        cols = pl.ds(pl.multiple_of(pair * 256, 256), 256)
+        return remote(
+            sk.at[:, cols], rk.at[:, cols], kv_send.at[0], kv_recv.at[0, pair], seq_2=other
+        )
+
+    def value_copy(pair):
+        cols = pl.ds(pl.multiple_of(pair * 128, 128), 128)
+        return remote(
+            sv.at[:, cols], rv.at[:, cols], kv_send.at[1], kv_recv.at[1, pair], seq_2=other
+        )
+
     for load in loads[:3]:
         load.wait()
     ds_row = jnp.broadcast_to(ds_in[...].astype(F32), (8, 128))
@@ -116,13 +135,15 @@
     loads[4].wait()
     sv[...] = v_in[:, v_cols].astype(F32)
     pl.semaphore_wait(barrier, 13)
-    for swap in swaps[:3]:
-        swap.start()
+    swaps[0].start()
+    for n in (2, 1, 3, 0):
+        key_copy((y + n) % 4).start()
+        value_copy((y + n) % 4).start()
     loads[5].wait()
     sg[...] = g_in[:, v_cols].astype(F32)
     loads[6].wait()
     sq[...] = q_in[:, q_cols].astype(F32)
-    for swap in swaps[3:]:
+    for swap in swaps[1:]:
         swap.start()
     kb[own_rows, :] = k_in[:, own_q]
     vb[own_rows, :] = v_in[:, own_v]
@@ -189,7 +210,7 @@
         rows = 136 if kind == 0 else 128
         return remote(
             ys.at[pair, kind, pl.ds(0, rows)], yr.at[at_y, kind, pl.ds(0, rows)],
-            y1_send.at[pair, kind], y1_recv.at[at_y, kind], seq_1=pair,
+            y1_send.at[kind], y1_recv.at[kind], seq_1=pair,
         )
 
     def place(pair, kind, i, slab):
@@ -209,6 +230,11 @@
             y1_copy(pair, kind, y).start()
 
     def state_fwd(pair):
+        wide = pl.ds(pl.multiple_of(pair * 256, 256), 256)
+        key_copy(pair).wait_recv()
+        kb[other_rows, wide] = rk[:, wide].astype(BF16)
+        value_copy(pair).wait_recv()
+        vb[other_rows, pair_cols(pair)] = rv[:, pair_cols(pair)].astype(BF16)
         vt[pair] = jnp.transpose(vb[:, pair_cols(pair)].astype(F32))
         for i in range(2):
             head = pl.ds(pair * 2 + i, 1)
@@ -311,7 +337,7 @@
 
     def y2_copy(to_y, kind, src):
         return remote(
-            src, zr.at[y, kind], y2_send.at[to_y, kind], y2_recv.at[y, kind], seq_1=to_y
+            src, zr.at[y, kind], y2_send.at[kind], y2_recv.at[y, kind // 3], seq_1=to_y
         )
 
     def y2_source(to_y, kind):
@@ -334,15 +360,27 @@
         else:
             go()
 
+    def several(buf, count, kind, send, recv):
+        rows = pl.ds(0, 136 if kind == 0 and buf is ys else 128)
+        return remote(
+            buf.at[pl.ds(0, count), kind, rows], buf.at[pl.ds(0, count), kind, rows],
+            send, recv, seq_2=other,
+        )
+
+    def in_turn(kind, here, act):
+        pl.when(here)(lambda: act(1))
+        pl.when(jnp.logical_not(here))(lambda: act(2))
+
     def y1_wait(kind):
-        for at_y in range(4):
-            here = sent(kind, at_y)
-            if here is False:
-                continue
-
-            @pl.when((y != at_y) & here)
-            def _():
-                y1_copy(y, kind, at_y).wait_recv()
+        def act(count):
+            several(ys, count, kind, y1_send.at[kind], y1_recv.at[kind]).wait_recv()
+
+        if kind == 0:
+            act(3)
+        elif kind == 1:
+            pl.when(x > 0)(lambda: act(3))
+        else:
+            in_turn(kind, y % 2 == 1 if kind == 2 else y >= 2, act)
 
     def x_copy(to_x, kind):
         return remote(xs.at[kind], xr.at[x], x_send.at[to_x], x_recv.at[x], seq_0=to_x)
@@ -443,19 +481,18 @@
             out_send.at[kind], out_recv.at[kind], seq_2=other,
         )
 
-    def y2_wait(pair, kinds):
-        for kind in kinds:
-            here = (y % 2 == 1, y >= 2, x > 0, True)[kind]
-
-            @pl.when((pair != y) & here)
-            def _():
-                remote(
-                    zs.at[0, kind], zr.at[pair, kind], y2_send.at[0, kind],
-                    y2_recv.at[pair, kind], seq_1=pair,
-                ).wait_recv()
+    def y2_wait(pair, first, count):
+        remote(
+            zr.at[pair, pl.ds(0, count)], zr.at[pair, pl.ds(0, count)], y2_send.at[0],
+            y2_recv.at[pair, first // 3], seq_1=pair,
+        ).wait_recv()
 
     def cross_in(pair):
-        y2_wait(pair, (0, 1, 2))
+        levels_in = y % 2 + y // 2 + (x > 0).astype(jnp.int32)
+        for count in range(1, 4):
+            pl.when((pair != y) & (levels_in == count))(
+                functools.partial(y2_wait, pair, 0, count)
+            )
         for i in range(2):
             head = pl.ds(pair * 2 + i, 1)
             rows = pl.ds(64 * i, 64)
@@ -488,7 +525,7 @@
         gq_out[:, out_wide] = gq[own_rows, wide].astype(BF16)
 
     def cross_out(pair):
-        y2_wait(pair, (3,))
+        pl.when(pair != y)(functools.partial(y2_wait, pair, 3, 1))
         for i in range(2):
             head = pl.ds(pair * 2 + i, 1)
             rows = pl.ds(64 * i, 64)
@@ -528,20 +565,10 @@
 
         lax.fori_loop(low, high, step, 0)
 
-    def toward(n):
-        return (y + jnp.where(n == 2, 3, jnp.where(n == 3, 0, 2 - n))) % 4
-
-    def nearby(n):
-        return (y + jnp.where(n == 2, 3, jnp.where(n == 3, 2, n))) % 4
-
+    loop(0, 4, lambda n: state_fwd(toward(n)))
     swaps[1].wait_recv()
-    kb[other_rows, :] = rk[...].astype(BF16)
+    gb[other_rows, :] = rg[...].astype(BF16)
     swaps[2].wait_recv()
-    vb[other_rows, :] = rv[...].astype(BF16)
-    loop(0, 4, lambda n: state_fwd(toward(n)))
-    swaps[3].wait_recv()
-    gb[other_rows, :] = rg[...].astype(BF16)
-    swaps[4].wait_recv()
     qb[other_rows, :] = rq[...].astype(BF16)
     loop(0, 4, lambda n: state_back(toward(n)))
     loop(0, 4, lambda n: state_near(toward(n)))
@@ -645,20 +672,23 @@
 
     for swap in swaps:
         swap.wait_send()
+    remote(sk, rk, kv_send.at[0], kv_recv.at[0, 0], seq_2=other).wait_send()
+    remote(sv, rv, kv_send.at[1], kv_recv.at[1, 0], seq_2=other).wait_send()
+    for kind in range(4):
+
+        @pl.when(sent(kind, y))
+        def _():
+            several(ys, 3, kind, y1_send.at[kind], y1_recv.at[kind]).wait_send()
+
+        def act(count):
+            several(zs, count, kind, y2_send.at[kind], y2_recv.at[0, 0]).wait_send()
+
+        if kind < 2:
+            in_turn(kind, y % 2 == 1 if kind == 0 else y >= 2, act)
+        else:
+            pl.when(x > 0 if kind == 2 else y >= 0)(lambda: act(3))
+
     for pair in range(4):
-        for kind in range(4):
-
-            @pl.when((y != pair) & sent(kind, y))
-            def _():
-                y1_copy(pair, kind, y).wait_send()
-
-            back = (pair % 2 == 1, pair >= 2, x > 0, True)[kind]
-            if back is not False:
-
-                @pl.when((y != pair) & back)
-                def _():
-                    y2_copy(pair, kind, y2_source(pair, kind)).wait_send()
-
         @pl.when(pair != x)
         def _():
             x_copy(pair, 0).wait_send()
@@ -712,7 +742,7 @@
     scratch += [pltpu.VMEM((128, 1024), F32), pltpu.VMEM((128, 1024), F32), pltpu.VMEM((128, 512), F32)]
     scratch += [pltpu.VMEM((56, 128), F32)]
     scratch += [pltpu.VMEM((128, 1, 128), F32)]
-    sems = [(5,), (5,), (4, 4), (4, 4), (4, 4), (4, 4), (4,), (4,), (3,), (3,), (2,), (2,)]
+    sems = [(3,), (3,), (2,), (2, 4), (4,), (4,), (4,), (4, 2), (4,), (4,), (3,), (3,), (2,), (2,)]
     sems += [(1,)] * 2
     scratch += [pltpu.SemaphoreType.DMA(s) for s in sems]
     outs = pl.pallas_call(

time: 42.5 us -> 41.7 us (0.981)
  Pallas kernels: 41.8 us -> 40.9 us
    pallas_call x1, Pallas kernels: 40.6 us -> 39.7 us  [shards(): pl.pallas_call(kernel, out_shape=held, in_specs=[anywhere] * 7, out_specs...]
where the time goes in v6:
time: 41.7 us; the launch traced here: 41.5 us
  Pallas kernels  40.9 us (98%)
  between operations  0.64 us (2%)
    pallas_call x1, Pallas kernels, shards(): pl.pallas_call(kernel, out_shape=held, in_specs=[anywhere] * 7, out_specs...  39.7 us
    pallas_call x1, Pallas kernels, shards(): pl.pallas_call(settle, out_shape=results, in_specs=[anywhere] * 5, out_sp...  1.16 us

profile of v6, /device:TPU:1, one launch (start us, length us, event | category | flops | bytes accessed | tf_op | source)
XLA Modules:
  0.0 41.5 jit_solution(17471624140052486133)
XLA Ops:
  0.6 39.7 %shard_map.110 = (bf16[128,2048]{1,0:T(8,128)(2,1)S(1)}, bf16[128,2048]{1,0:T(8,128)(2,1)S(1)}, bf16[128,1024]{1,0:T(8,128)(2,1)S(1)}, f32[6,16,128]{2,1,0:T(8,128)S(1)}, f32[16,128]{1,0:T(8,128)S(1)}) custom-call(bf16[128,2048]{1,0:T(8,128)(2,1)} %q_hbm.1, bf16[128,2048]{1,0:T(8,128)(2,1)} %k_hbm.1, bf16[128,1024]{1,0:T(8,128)(2,1)} %v_hbm.1, ...), custom_call_target="tpu_custom_call" | custom-call | tf_op jit(solution)/shard_map/pallas_call | solution.py:748
  40.4 1.2 %shard_map.111 = (bf16[128,2048]{1,0:T(8,128)(2,1)}, bf16[128,2048]{1,0:T(8,128)(2,1)}, bf16[128,1024]{1,0:T(8,128)(2,1)}, f32[6,16,128]{2,1,0:T(8,128)}, f32[16,128]{1,0:T(8,128)}) custom-call(bf16[128,2048]{1,0:T(8,128)(2,1)S(1)} %get-tuple-element.10.refs_0_, bf16[128,2048]{1,0:T(8,128)(2,1)S(1)} %get-tuple-element.11.refs_1_, ...), custom_call_target="tpu_custom_call" | custom-call | tf_op jit(solution)/shard_map/pallas_call | solution.py:758

commit v7 on v6

--- a/solution.py
+++ b/solution.py
@@ -86,11 +86,10 @@
             pl.semaphore_signal(
                 barrier, inc=1, device_id={axis: (place + step) % 4}, device_id_type=MESH
             )
-    for step in range(1, 8):
-        peer = (group + step) % 8
         pl.semaphore_signal(
-            barrier, inc=1, device_id={"head": peer // 2, "seq_2": peer % 2}, device_id_type=MESH
-        )
+            barrier, inc=1, device_id={"head": (z + step) % 4}, device_id_type=MESH
+        )
+    pl.semaphore_signal(barrier, inc=1, device_id={"seq_2": other}, device_id_type=MESH)
 
     q_cols = pl.ds(pl.multiple_of(other * 1024, 1024), 1024)
     v_cols = pl.ds(pl.multiple_of(other * 512, 512), 512)
@@ -134,7 +133,7 @@
     sk[...] = k_in[:, q_cols].astype(F32)
     loads[4].wait()
     sv[...] = v_in[:, v_cols].astype(F32)
-    pl.semaphore_wait(barrier, 13)
+    pl.semaphore_wait(barrier, 10)
     swaps[0].start()
     for n in (2, 1, 3, 0):
         key_copy((y + n) % 4).start()
@@ -510,19 +509,6 @@
                 glw[3 + n, head, :] = level_row
                 drift_row = drift_row + wts[3 + n, head, :] * level_row
             drift[head, :] = drift_row
-            weighted_hi, weighted_lo = split(
-                jnp.concatenate(
-                    [grad * (fs[head, :] * wts[3 + n, head, :]) for n in range(3)], axis=0
-                )
-            )
-            gq[:, head_cols(pair, i)] = gq[:, head_cols(pair, i)] + dot(
-                jnp.concatenate([weighted_hi, weighted_lo, weighted_hi], axis=0),
-                jnp.concatenate([enter_hi, enter_hi, enter_lo], axis=0), TN,
-            )
-        back_copy(pair, 0).start()
-        wide = pl.ds(pl.multiple_of(pair * 256, 256), 256)
-        out_wide = pl.ds(pl.multiple_of(c * 1024 + pair * 256, 256), 256)
-        gq_out[:, out_wide] = gq[own_rows, wide].astype(BF16)
 
     def cross_out(pair):
         pl.when(pair != y)(functools.partial(y2_wait, pair, 3, 1))
@@ -538,6 +524,27 @@
             drift[head, :] = drift[head, :] - jnp.sum(
                 vt[pair, rows] * value_grad, axis=0, keepdims=True
             )
+
+    def cross_query(pair):
+        for i in range(2):
+            head = pl.ds(pair * 2 + i, 1)
+            rows = pl.ds(64 * i, 64)
+            enter_hi, enter_lo = split(
+                jnp.concatenate([zr[pair, n, rows] for n in range(3)], axis=0)
+            )
+            weighted_hi, weighted_lo = split(
+                jnp.concatenate(
+                    [gt[pair, rows] * (fs[head, :] * wts[3 + n, head, :]) for n in range(3)], axis=0
+                )
+            )
+            gq[:, head_cols(pair, i)] = gq[:, head_cols(pair, i)] + dot(
+                jnp.concatenate([weighted_hi, weighted_lo, weighted_hi], axis=0),
+                jnp.concatenate([enter_hi, enter_hi, enter_lo], axis=0), TN,
+            )
+        back_copy(pair, 0).start()
+        wide = pl.ds(pl.multiple_of(pair * 256, 256), 256)
+        out_wide = pl.ds(pl.multiple_of(c * 1024 + pair * 256, 256), 256)
+        gq_out[:, out_wide] = gq[own_rows, wide].astype(BF16)
 
     def cross_grad(pair):
         for i in range(2):
@@ -576,9 +583,9 @@
     masks()
     loop(0, 1, intra)
     combine_back()
-    loop(1, 3, intra)
+    loop(1, 2, intra)
     enter_far()
-    loop(3, 4, intra)
+    loop(2, 4, intra)
     leave_far()
     loop(0, 4, lambda n: cross_in(nearby(n)))
     loop(0, 4, lambda n: cross_out(nearby(n)))
@@ -624,6 +631,7 @@
     for level in range(6):
         glw_out[level, own_heads, :] = glw[level, :, own_rows]
 
+    loop(0, 4, cross_query)
     loop(0, 4, cross_grad)
     def back_whole(kind):
         src, dst = ((gq, bq), (gk, bk), (gv, bv))[kind]

time: 41.7 us -> 41.2 us (0.988)
  Pallas kernels: 40.9 us -> 40.4 us
    pallas_call x1, Pallas kernels: 39.7 us -> 39.2 us  [shards(): pl.pallas_call(kernel, out_shape=held, in_specs=[anywhere] * 7, out_specs...]
where the time goes in v7:
time: 41.2 us; the launch traced here: 41 us
  Pallas kernels  40.4 us (98%)
  between operations  0.64 us (2%)
    pallas_call x1, Pallas kernels, shards(): pl.pallas_call(kernel, out_shape=held, in_specs=[anywhere] * 7, out_specs...  39.2 us
    pallas_call x1, Pallas kernels, shards(): pl.pallas_call(settle, out_shape=results, in_specs=[anywhere] * 5, out_sp...  1.16 us

profile of v7, /device:TPU:1, one launch (start us, length us, event | category | flops | bytes accessed | tf_op | source)
XLA Modules:
  0.0 41.0 jit_solution(5034029983868959826)
XLA Ops:
  0.6 39.2 %shard_map.110 = (bf16[128,2048]{1,0:T(8,128)(2,1)S(1)}, bf16[128,2048]{1,0:T(8,128)(2,1)S(1)}, bf16[128,1024]{1,0:T(8,128)(2,1)S(1)}, f32[6,16,128]{2,1,0:T(8,128)S(1)}, f32[16,128]{1,0:T(8,128)S(1)}) custom-call(bf16[128,2048]{1,0:T(8,128)(2,1)} %q_hbm.1, bf16[128,2048]{1,0:T(8,128)(2,1)} %k_hbm.1, bf16[128,1024]{1,0:T(8,128)(2,1)} %v_hbm.1, ...), custom_call_target="tpu_custom_call" | custom-call | tf_op jit(solution)/shard_map/pallas_call | solution.py:756
  39.9 1.2 %shard_map.111 = (bf16[128,2048]{1,0:T(8,128)(2,1)}, bf16[128,2048]{1,0:T(8,128)(2,1)}, bf16[128,1024]{1,0:T(8,128)(2,1)}, f32[6,16,128]{2,1,0:T(8,128)}, f32[16,128]{1,0:T(8,128)}) custom-call(bf16[128,2048]{1,0:T(8,128)(2,1)S(1)} %get-tuple-element.10.refs_0_, bf16[128,2048]{1,0:T(8,128)(2,1)S(1)} %get-tuple-element.11.refs_1_, ...), custom_call_target="tpu_custom_call" | custom-call | tf_op jit(solution)/shard_map/pallas_call | solution.py:766

commit v8 on v7

--- a/solution.py
+++ b/solution.py
@@ -406,8 +406,10 @@
             def _():
                 x_copy(to_x, 0).start()
 
-        hand_back(1, 0)
-        hand_back(3, 0)
+        @pl.when(y % 2 == 1)
+        def _():
+            zr[y, 0] = yr[(y + 3) % 4, 0, 0:128]
+
         hand_back(2, 1)
         hand_back(3, 1)
 
@@ -429,6 +431,20 @@
             def _():
                 x_copy(to_x, 1).start()
 
+
+    def next_copy(pair, src):
+        return remote(
+            src, zr.at[pair, 0], y2_send.at[0], y2_recv.at[pair, 0], seq_1=(y + 1) % 4
+        )
+
+    def hand_next(pair):
+        @pl.when((y % 2 == 0) & (pair == y))
+        def _():
+            next_copy(pair, yr.at[y, 0, pl.ds(0, 128)]).start()
+
+        @pl.when((y % 2 == 0) & (pair != y) & (pair != y + 1))
+        def _():
+            next_copy(pair, ys.at[pair, 0, pl.ds(0, 128)]).start()
 
     def take(acc, at_x):
         remote(
@@ -579,6 +595,7 @@
     qb[other_rows, :] = rq[...].astype(BF16)
     loop(0, 4, lambda n: state_back(toward(n)))
     loop(0, 4, lambda n: state_near(toward(n)))
+    loop(0, 4, hand_next)
     combine_fwd()
     masks()
     loop(0, 1, intra)
@@ -691,8 +708,10 @@
         def act(count):
             several(zs, count, kind, y2_send.at[kind], y2_recv.at[0, 0]).wait_send()
 
-        if kind < 2:
-            in_turn(kind, y % 2 == 1 if kind == 0 else y >= 2, act)
+        if kind == 0:
+            pl.when(y % 2 == 0)(lambda: act(3))
+        elif kind == 1:
+            in_turn(kind, y >= 2, act)
         else:
             pl.when(x > 0 if kind == 2 else y >= 0)(lambda: act(3))
 

time: 41.2 us -> 40.2 us (0.976)
  Pallas kernels: 40.4 us -> 39.4 us
    pallas_call x1, Pallas kernels: 39.2 us -> 38.2 us  [shards(): pl.pallas_call(kernel, out_shape=held, in_specs=[anywhere] * 7, out_specs...]
where the time goes in v8:
time: 40.2 us; the launch traced here: 40 us
  Pallas kernels  39.4 us (98%)
  between operations  0.64 us (2%)
    pallas_call x1, Pallas kernels, shards(): pl.pallas_call(kernel, out_shape=held, in_specs=[anywhere] * 7, out_specs...  38.2 us
    pallas_call x1, Pallas kernels, shards(): pl.pallas_call(settle, out_shape=results, in_specs=[anywhere] * 5, out_sp...  1.16 us

profile of v8, /device:TPU:1, one launch (start us, length us, event | category | flops | bytes accessed | tf_op | source)
XLA Modules:
  0.0 40.0 jit_solution(6029284776238779574)
XLA Ops:
  0.6 38.2 %shard_map.110 = (bf16[128,2048]{1,0:T(8,128)(2,1)S(1)}, bf16[128,2048]{1,0:T(8,128)(2,1)S(1)}, bf16[128,1024]{1,0:T(8,128)(2,1)S(1)}, f32[6,16,128]{2,1,0:T(8,128)S(1)}, f32[16,128]{1,0:T(8,128)S(1)}) custom-call(bf16[128,2048]{1,0:T(8,128)(2,1)} %q_hbm.1, bf16[128,2048]{1,0:T(8,128)(2,1)} %k_hbm.1, bf16[128,1024]{1,0:T(8,128)(2,1)} %v_hbm.1, ...), custom_call_target="tpu_custom_call" | custom-call | tf_op jit(solution)/shard_map/pallas_call | solution.py:775
  38.9 1.2 %shard_map.111 = (bf16[128,2048]{1,0:T(8,128)(2,1)}, bf16[128,2048]{1,0:T(8,128)(2,1)}, bf16[128,1024]{1,0:T(8,128)(2,1)}, f32[6,16,128]{2,1,0:T(8,128)}, f32[16,128]{1,0:T(8,128)}) custom-call(bf16[128,2048]{1,0:T(8,128)(2,1)S(1)} %get-tuple-element.10.refs_0_, bf16[128,2048]{1,0:T(8,128)(2,1)S(1)} %get-tuple-element.11.refs_1_, ...), custom_call_target="tpu_custom_call" | custom-call | tf_op jit(solution)/shard_map/pallas_call | solution.py:785

commit v9 on v8

--- a/solution.py
+++ b/solution.py
@@ -731,7 +731,7 @@
     source, target, sem = refs[:5], refs[5:10], refs[10]
     stores = []
     for n in range(5):
-        cuts = 4 if n < 2 else 2 if n == 2 else 1
+        cuts = 1
         rows = source[n].shape[0] // cuts
         for m in range(cuts):
             at = pl.ds(rows * m, rows)

time: 40.2 us -> 40.2 us (level)
  no operation moved by 1% of the time
where the time goes in v9:
time: 40.2 us; the launch traced here: 40 us
  Pallas kernels  39.4 us (98%)
  between operations  0.64 us (2%)
    pallas_call x1, Pallas kernels, shards(): pl.pallas_call(kernel, out_shape=held, in_specs=[anywhere] * 7, out_specs...  38.2 us
    pallas_call x1, Pallas kernels, shards(): pl.pallas_call(settle, out_shape=results, in_specs=[anywhere] * 5, out_sp...  1.16 us

profile of v9, /device:TPU:1, one launch (start us, length us, event | category | flops | bytes accessed | tf_op | source)
XLA Modules:
  0.0 40.0 jit_solution(11612836050112571302)
XLA Ops:
  0.6 38.2 %shard_map.110 = (bf16[128,2048]{1,0:T(8,128)(2,1)S(1)}, bf16[128,2048]{1,0:T(8,128)(2,1)S(1)}, bf16[128,1024]{1,0:T(8,128)(2,1)S(1)}, f32[6,16,128]{2,1,0:T(8,128)S(1)}, f32[16,128]{1,0:T(8,128)S(1)}) custom-call(bf16[128,2048]{1,0:T(8,128)(2,1)} %q_hbm.1, bf16[128,2048]{1,0:T(8,128)(2,1)} %k_hbm.1, bf16[128,1024]{1,0:T(8,128)(2,1)} %v_hbm.1, ...), custom_call_target="tpu_custom_call" | custom-call | tf_op jit(solution)/shard_map/pallas_call | solution.py:775
  38.9 1.2 %shard_map.111 = (bf16[128,2048]{1,0:T(8,128)(2,1)}, bf16[128,2048]{1,0:T(8,128)(2,1)}, bf16[128,1024]{1,0:T(8,128)(2,1)}, f32[6,16,128]{2,1,0:T(8,128)}, f32[16,128]{1,0:T(8,128)}) custom-call(bf16[128,2048]{1,0:T(8,128)(2,1)S(1)} %get-tuple-element.10.refs_0_, bf16[128,2048]{1,0:T(8,128)(2,1)S(1)} %get-tuple-element.11.refs_1_, ...), custom_call_target="tpu_custom_call" | custom-call | tf_op jit(solution)/shard_map/pallas_call | solution.py:785
